TPU v7x, 32 devices: a whole 2x2x4 slice. The times are simulated.
32 devices in a mesh: mem: 4 (over z), hor: 2 (over x), grp: 4 (over y, core).
Axes of the slice: x: 2, y: 2, z: 4, core: 2. Of those that a mesh axis runs over, the one named last changes fastest.
Arguments:
- ensemble: float32 [128, 2, 32, 1024], P(('mem', 'grp'), None, None, 'hor'), may hold values from -1 to 1
- coupling: float32 [32, 32], replicated, may hold values from -1 to 1
- obs_column: int32 [2, 16, 2, 512], P(None, ('mem', 'grp'), 'hor'), may hold values from 0 to 511
- obs_level: int32 [2, 16, 2, 512], P(None, ('mem', 'grp'), 'hor'), may hold values from 0 to 1
- obs_value: float32 [2, 16, 2, 512], P(None, ('mem', 'grp'), 'hor'), may hold values from -6 to 6
- obs_error: float32 [2, 16, 2, 512], P(None, ('mem', 'grp'), 'hor'), may hold values from 0.25 to 4
- obs_live: int32 [2, 16, 2, 512], P(None, ('mem', 'grp'), 'hor'), may hold values 0 or 1
- partners: int32 [16, 2, 2], P(('mem', 'grp'), 'hor'), may hold values from 0 to 15, as said below
Outputs:
- analysed: float32 [128, 2, 32, 1024], P(('mem', 'grp'), None, None, 'hor')
Inputs may be any that keep to these rules, and one draw needn't show every extreme that they name: `partners`: each row holds 2 different slab numbers, none of them the row's own slab.
All inputs are finite; a program needn't handle non-finite values. No bound on the sum of `obs_live` on one device may be relied on, other than what follows from the above.
Results may differ from a plain program's by a relative error of at most 0.0003.
Values sent between devices are 32-bit elements; how exact they have to be, the bound alone decides.
A program may use at most 64 MiB of HBM per device.

v0:
```python
import functools

import jax
import jax.numpy as jnp
from jax import lax
from jax.experimental import pallas as pl
from jax.experimental.pallas import tpu as pltpu
from jax.sharding import PartitionSpec as P

SUBSTEPS = 4
ROOT_STEPS = 8
MESH = pl.DeviceIdType.MESH


time_step = 0.2


def sent(piece, axis, pairs):
    width = piece.shape[-1]
    packed = jnp.moveaxis(piece, -1, 0).reshape(width, -1)
    moved = lax.ppermute(packed, axis, pairs)
    return jnp.moveaxis(moved.reshape((width,) + piece.shape[:-1]), 0, -1)


def with_halo(block, axis, width):
    count = lax.axis_size(axis)
    forward = [(i, (i + 1) % count) for i in range(count)]
    backward = [(target, source) for source, target in forward]
    low = sent(block[..., block.shape[-1] - width :], axis, forward)
    high = sent(block[..., :width], axis, backward)
    return jnp.concatenate([low, block, high], axis=-1)


def centred(field):
    return (field[..., 2:] - field[..., :-2]) * 0.5


def substep(velocity, height, coupling):
    pressure = jnp.einsum("lk,mkc->mlc", coupling, height, precision=lax.Precision.HIGHEST)
    inner = velocity[..., 1:-1]
    moved = inner - time_step * (inner * centred(velocity) + centred(pressure))
    fluxes = moved * height[..., 1:-1]
    height_new = height[..., 2:-2] - time_step * centred(fluxes)
    return (moved[..., 1:-1], height_new)


def advance(members, coupling):
    extended = with_halo(members, "hor", 2 * SUBSTEPS)
    velocity, height = (extended[:, 0], extended[:, 1])
    for step_index in range(SUBSTEPS):
        velocity, height = substep(velocity, height, coupling)
    return velocity, height


def to_slabs(field, slab_count):
    block, levels, cells = field.shape
    return field.reshape(block, slab_count, -1).transpose(1, 0, 2)


def split(value):
    high = value.astype(jnp.bfloat16)
    return high, (value - high.astype(jnp.float32)).astype(jnp.bfloat16)


def product(left, right, across=0):
    dims = (((1,), (across,)), ((), ()))

    def one(a, b):
        return lax.dot_general(a, b, dims, preferred_element_type=jnp.float32)

    left_high, left_low = split(left)
    right_high, right_low = split(right)
    return one(left_high, right_high) + (one(left_high, right_low) + one(left_low, right_high))


def analysis(
    sizes, count,
    seen_ref, value_ref, error_ref, live_ref, blend_ref, height_ref, velocity_ref, out_ref,
    own, column, partial, arrived, peers_blend, gathered, updated, returned,
    send_a, recv_a, send_b, recv_b, send_c, recv_c, send_d, recv_d, send_e, recv_e,
):
    mem_count, grp_count = sizes
    mem = lax.axis_index("mem")
    grp = lax.axis_index("grp")

    def mem_peer(step):
        return lax.rem(mem + step, mem_count)

    def grp_peer(step):
        return lax.rem(grp + step, grp_count)

    barrier = pltpu.get_barrier_semaphore()
    slab = mem * grp_count + grp
    peers = []
    for mem_step in range(mem_count):
        for grp_step in range(grp_count):
            if mem_step + grp_step > 0:
                peers.append((mem_peer(mem_step), grp_peer(grp_step)))
    for one, other in peers:
        pl.semaphore_signal(
            barrier, inc=1, device_id={"mem": one, "grp": other}, device_id_type=MESH
        )

    def exchange(source, target, send_sem, recv_sem):
        copies = []
        for at, (one, other) in enumerate(peers):
            copy = pltpu.make_async_remote_copy(
                src_ref=source.at[one * grp_count + other], dst_ref=target.at[slab],
                send_sem=send_sem.at[at], recv_sem=recv_sem.at[at],
                device_id={"mem": one, "grp": other}, device_id_type=MESH,
            )
            copy.start()
            copies.append(copy)
        return copies


    width = seen_ref.shape[0]
    seen = seen_ref[...]
    average = jnp.mean(seen, axis=0, keepdims=True)
    anomalies = seen - average
    weight = live_ref[...].astype(jnp.float32) / error_ref[...]
    pull = weight * (value_ref[...] - average)
    rows = jnp.concatenate(
        [anomalies * weight, jnp.broadcast_to(pull, (8, pull.shape[1]))], axis=0
    )
    own[...] = product(rows, anomalies, 1)

    pl.semaphore_wait(barrier, mem_count * grp_count - 1)
    blends = []
    for step in range(1, grp_count):
        copy = pltpu.make_async_remote_copy(
            src_ref=blend_ref, dst_ref=peers_blend.at[step - 1],
            send_sem=send_b.at[step - 1], recv_sem=recv_b.at[step - 1],
            device_id={"grp": grp_peer(step)}, device_id_type=MESH,
        )
        copy.start()
        blends.append(copy)
    gathers = []
    for step in range(1, mem_count):
        copy = pltpu.make_async_remote_copy(
            src_ref=own, dst_ref=column.at[step - 1],
            send_sem=send_a.at[step - 1], recv_sem=recv_a.at[step - 1],
            device_id={"mem": mem_peer(step)}, device_id_type=MESH,
        )
        copy.start()
        gathers.append(copy)
    for copy in blends:
        copy.wait()
    lanes = lax.broadcasted_iota(jnp.int32, (1, blend_ref.shape[1]), 1)

    def share(row, step):
        place = lax.rem(mem + mem_count - step, mem_count) * grp_count + grp
        return jnp.sum(jnp.where(lanes == place, row[0:1], 0.0), axis=1, keepdims=True)

    for copy in gathers:
        copy.wait()

    def blended_for(row):
        total = share(row, 0) * own[...]
        for step in range(1, mem_count):
            total = total + share(row, step) * column[step - 1]
        return total

    returns = []
    for step in range(1, grp_count):
        partial[step - 1] = blended_for(peers_blend[step - 1])
        copy = pltpu.make_async_remote_copy(
            src_ref=partial.at[step - 1], dst_ref=arrived.at[step - 1],
            send_sem=send_c.at[step - 1], recv_sem=recv_c.at[step - 1],
            device_id={"grp": grp_peer(grp_count - step)}, device_id_type=MESH,
        )
        copy.start()
        returns.append(copy)
    total = blended_for(blend_ref[...])
    outward = exchange(velocity_ref, gathered, send_d, recv_d)
    gathered[slab] = velocity_ref[slab]
    for copy in returns:
        copy.wait()
    for step in range(1, grp_count):
        total = total + arrived[step - 1]

    total = total / (count + 1.0)
    square = (width, width)
    identity = (
        lax.broadcasted_iota(jnp.int32, square, 0) == lax.broadcasted_iota(jnp.int32, square, 1)
    ).astype(jnp.float32)
    blended = (width - 1.0) * identity + total[:width]
    bvector = total[width:]
    squares = jnp.sum(jnp.sum(blended * blended, axis=1, keepdims=True), axis=0, keepdims=True)
    frobenius = jnp.sqrt(squares)
    iterate = blended / frobenius
    newton = 1.5 * identity - 0.5 * iterate
    inverse_root = newton
    for step in range(1, ROOT_STEPS):
        iterate = product(newton, iterate)
        newton = 1.5 * identity - 0.5 * product(inverse_root, iterate)
        inverse_root = product(newton, inverse_root)
    spread = inverse_root * (jnp.sqrt(width - 1.0) / jnp.sqrt(frobenius))
    inner = product(bvector, inverse_root)
    mean_weight = product(inner, inverse_root) / frobenius
    transposed = spread + mean_weight[0:1]

    def update(flat, field):
        flat_average = jnp.mean(flat, axis=0, keepdims=True)
        result = flat_average + product(transposed, flat - flat_average)
        updated[field] = result.reshape(updated.shape[1:])
        copies = exchange(updated.at[field], returned.at[field], send_e.at[field], recv_e.at[field])
        returned[field, slab] = updated[field, slab]
        return copies

    back = update(height_ref[...], 1)
    for copy in outward:
        copy.wait()
    back = back + update(gathered[...].reshape(height_ref.shape), 0)
    for copy in back:
        copy.wait()
    out_ref[...] = returned[...]


def analysed(sizes, count, seen, value, error, live, blend, height, velocity):
    width = seen.shape[0]
    mem_count, grp_count = sizes
    tall = (width + 8, width)
    vmem = pl.BlockSpec(memory_space=pltpu.VMEM)
    dma = pltpu.SemaphoreType.DMA
    return pl.pallas_call(
        functools.partial(analysis, sizes, count),
        out_shape=jax.ShapeDtypeStruct((2,) + velocity.shape, jnp.float32),
        in_specs=[vmem] * 7,
        out_specs=vmem,
        scratch_shapes=[
            pltpu.VMEM(tall, jnp.float32),
            pltpu.VMEM((mem_count - 1,) + tall, jnp.float32),
            pltpu.VMEM((grp_count - 1,) + tall, jnp.float32),
            pltpu.VMEM((grp_count - 1,) + tall, jnp.float32),
            pltpu.VMEM((grp_count - 1,) + blend.shape, jnp.float32),
            pltpu.VMEM(velocity.shape, jnp.float32),
            pltpu.VMEM((2,) + velocity.shape, jnp.float32),
            pltpu.VMEM((2,) + velocity.shape, jnp.float32),
            dma((mem_count - 1,)), dma((mem_count - 1,)),
            dma((grp_count - 1,)), dma((grp_count - 1,)),
            dma((grp_count - 1,)), dma((grp_count - 1,)),
            dma((mem_count * grp_count - 1,)), dma((mem_count * grp_count - 1,)),
            dma((2, mem_count * grp_count - 1)), dma((2, mem_count * grp_count - 1)),
        ],
        compiler_params=pltpu.CompilerParams(collective_id=0, has_side_effects=True),
    )(seen, value[None], error[None], live[None], blend, height, velocity)


def shards(ensemble, coupling, obs_column, obs_level, obs_value, obs_error, obs_live, partners):
    mem_count = lax.axis_size("mem")
    grp_count = lax.axis_size("grp")
    slab_count = mem_count * grp_count
    own_slab = lax.axis_index("mem") * grp_count + lax.axis_index("grp")
    lanes = max(128, -(-slab_count // 128) * 128)
    slab_numbers = jnp.arange(lanes, dtype=jnp.int32)
    chosen = partners[0, 0]
    count = chosen.shape[0]
    blend_weights = (slab_numbers == own_slab).astype(jnp.float32)
    blend_weights = blend_weights + jnp.sum(
        (slab_numbers[:, None] == chosen[None, :]).astype(jnp.float32), axis=1
    )
    blend = jnp.broadcast_to(blend_weights, (8, lanes))
    width = ensemble.shape[0] * slab_count
    cells = ensemble.shape[3]
    members = ensemble
    for cycle_index in range(obs_column.shape[0]):
        velocity, height = advance(members, coupling)
        heights = lax.all_to_all(
            to_slabs(height, slab_count), ("mem", "grp"), split_axis=0, concat_axis=0, tiled=True
        ).reshape(width, -1)
        place = obs_level[cycle_index, 0, 0] * cells + obs_column[cycle_index, 0, 0]
        observed = jnp.take(heights, place, axis=1)
        result = analysed(
            (mem_count, grp_count), count, observed,
            obs_value[cycle_index, 0, 0], obs_error[cycle_index, 0, 0],
            obs_live[cycle_index, 0, 0], blend, heights, to_slabs(velocity, slab_count),
        )
        shaped = result.reshape(2, slab_count, ensemble.shape[0], -1, cells)
        members = shaped.transpose(2, 0, 1, 3, 4).reshape(ensemble.shape)
    return members


def solution(mesh):
    in_specs = (
        P(("mem", "grp"), None, None, "hor"),
        P(),
        P(None, ("mem", "grp"), "hor", None),
        P(None, ("mem", "grp"), "hor", None),
        P(None, ("mem", "grp"), "hor", None),
        P(None, ("mem", "grp"), "hor", None),
        P(None, ("mem", "grp"), "hor", None),
        P(("mem", "grp"), "hor", None),
    )
    out_specs = P(("mem", "grp"), None, None, "hor")
    return jax.shard_map(shards, mesh=mesh, in_specs=in_specs, out_specs=out_specs, check_vma=False)
```

profile of v0, /device:TPU:11, one launch (start us, length us, event | category | flops | bytes accessed | tf_op | source)
XLA Modules:
  0.0 176.7 jit_solution(15209353822102408208)
XLA Ops:
  0.0 1.2 fusion.82
  1.8 1.3 collective-permute-start.1
  3.1 0.9 collective-permute-done
  5.3 0.7 convolution_bitcast_fusion.7
  5.9 0.7 slice_multiply_fusion.7
  7.8 0.9 slice_multiply_fusion.6
  9.8 0.9 slice_multiply_fusion.5
  11.8 0.9 slice_multiply_fusion.4
  13.3 1.1 copy.67
  14.4 8.0 %all-to-all-start = ((f32[16,8,1024]{2,1,0:T(8,128)}), f32[16,8,1024]{2,1,0:T(8,128)S(1)}, u32[]{:S(2)}, u32[]{:S(2)}) async-start(f32[16,8,1024]{2,1,0:T(8,128)} %bitcast.105), calls=%async_computation | async-start | bytes 1048576 | tf_op jit(solution)/shard_map/all_to_all | solution.py:269
  24.1 1.1 copy.66
  25.2 11.3 %all-to-all-done = f32[16,8,1024]{2,1,0:T(8,128)S(1)} async-done(((f32[16,8,1024]{2,1,0:T(8,128)}), f32[16,8,1024]{2,1,0:T(8,128)S(1)}, u32[]{:S(2)}, u32[]{:S(2)}) %all-to-all-start) | async-done | bytes 524320 | tf_op jit(solution)/shard_map/all_to_all | solution.py:269
  36.7 1.2 gather_fusion
  38.1 0.7 select_bitcast_fusion.1.seen_ref
  39.5 47.1 %shard_map.82 = f32[2,16,8,1024]{3,2,1,0:T(8,128)} custom-call(f32[128,512]{1,0:T(8,128)} %select_bitcast_fusion.1.seen_ref, f32[1,512]{1,0:T(1,128)} %get-tuple-element.38.value_ref, f32[1,512]{1,0:T(1,128)} %get-tuple-element.35.error_ref, s32[1,512]{1,0:T(1,128)} %get-tuple-element.33.live_ref, f32[8,128]{1,0:T(8,128)} %broadcast_in_dim.13.blend_ref, ...), custom_call_target="tpu_custom_call" | custom-call | tf_op jit(solution)/shard_map/pallas_call | solution.py:226
  86.6 1.8 %copy.56 = f32[8,2,32,512]{3,2,0,1:T(8,128)S(1)} copy(f32[8,2,32,512]{3,0,2,1:T(8,128)} %bitcast.111) | data formatting | bytes 2097152 | tf_op jit(solution)/shard_map/reshape | solution.py:280
  88.8 1.3 collective-permute-start.2
  90.6 0.8 collective-permute-done.2
  91.7 1.3 collective-permute-done.3
  93.8 0.7 convolution_bitcast_fusion.3
  94.5 0.7 slice_multiply_fusion.3
  96.3 0.9 slice_multiply_fusion.2
  98.4 0.9 slice_multiply_fusion.1
  100.4 1.1 slice_multiply_fusion
  102.1 1.1 copy.65
  103.2 7.4 %all-to-all-start.1 = ((f32[16,8,1024]{2,1,0:T(8,128)}), f32[16,8,1024]{2,1,0:T(8,128)S(1)}, u32[]{:S(2)}, u32[]{:S(2)}) async-start(f32[16,8,1024]{2,1,0:T(8,128)} %bitcast.103), calls=%async_computation.1 | async-start | bytes 1048576 | tf_op jit(solution)/shard_map/all_to_all | solution.py:269
  111.0 1.1 copy.64
  112.1 12.6 %all-to-all-done.1 = f32[16,8,1024]{2,1,0:T(8,128)S(1)} async-done(((f32[16,8,1024]{2,1,0:T(8,128)}), f32[16,8,1024]{2,1,0:T(8,128)S(1)}, u32[]{:S(2)}, u32[]{:S(2)}) %all-to-all-start.1) | async-done | bytes 524320 | tf_op jit(solution)/shard_map/all_to_all | solution.py:269
  124.9 1.0 gather_fusion.1
  126.1 0.7 select_bitcast_fusion.seen_ref
  126.8 47.1 %shard_map.83 = f32[2,16,8,1024]{3,2,1,0:T(8,128)} custom-call(f32[128,512]{1,0:T(8,128)} %select_bitcast_fusion.seen_ref, f32[1,512]{1,0:T(1,128)} %get-tuple-element.39.value_ref, f32[1,512]{1,0:T(1,128)} %get-tuple-element.34.error_ref, s32[1,512]{1,0:T(1,128)} %get-tuple-element.32.live_ref, f32[8,128]{1,0:T(8,128)} %broadcast_in_dim.13.blend_ref, ...), custom_call_target="tpu_custom_call" | custom-call | tf_op jit(solution)/shard_map/pallas_call | solution.py:226
  173.9 2.8 %copy.57 = f32[8,2,32,512]{3,2,1,0:T(8,128)} copy(f32[8,2,32,512]{3,0,2,1:T(8,128)} %bitcast.110) | data formatting | bytes 2097152 | tf_op jit(solution)/shard_map/reshape | solution.py:280
  (78 shorter events, 14.6 us)
Async XLA Ops:
  0.0 5.2 %copy-start = (f32[32,32]{1,0:T(8,128)S(1)}, f32[32,32]{1,0:T(8,128)}, u32[]{:S(2)}) copy-start(f32[32,32]{1,0:T(8,128)} %param.11) | copy-start | bytes 12292
  0.0 4.7 %copy-start.3 = (f32[8,2,32,512]{3,2,1,0:T(8,128)S(1)}, f32[8,2,32,512]{3,2,1,0:T(8,128)}, u32[]{:S(2)}) copy-start(f32[8,2,32,512]{3,2,1,0:T(8,128)} %param.10) | copy-start | bytes 3145732
  0.0 3.0 %copy-start.4 = (s32[2,1,1,512]{3,2,1,0:T(1,128)S(1)}, s32[2,1,1,512]{3,2,1,0:T(1,128)}, u32[]{:S(2)}) copy-start(s32[2,1,1,512]{3,2,1,0:T(1,128)} %param.12) | copy-start | bytes 12292
  0.0 3.0 %copy-start.5 = (s32[2,1,1,512]{3,2,1,0:T(1,128)S(1)}, s32[2,1,1,512]{3,2,1,0:T(1,128)}, u32[]{:S(2)}) copy-start(s32[2,1,1,512]{3,2,1,0:T(1,128)} %param.13) | copy-start | bytes 12292
  0.0 3.0 %copy-start.9 = (s32[1,1,2]{2,1,0:T(1,128)S(1)}, s32[1,1,2]{2,1,0:T(1,128)}, u32[]{:S(2)}) copy-start(s32[1,1,2]{2,1,0:T(1,128)} %param.17) | copy-start | bytes 28
  1.4 2.6 %collective-permute-start = (f32[8,512]{1,0:T(8,128)S(1)}, f32[8,512]{1,0:T(8,128)S(1)}, u32[]{:S(2)}, u32[]{:S(2)}) collective-permute-start(f32[8,512]{1,0:T(8,128)S(1)} %copy.37), channel_id=1, source_target_pairs={{0,4},{4,0},{1,5},{5,1},{2,6},{6,2},{3,7},{7,3},{8,12},{12,8},{9,1... | collective-permute-start | bytes 49160 | tf_op jit(solution)/shard_map/ppermute | solution.py:21
  1.8 2.6 %collective-permute-start.1 = (f32[8,512]{1,0:T(8,128)S(1)}, f32[8,512]{1,0:T(8,128)S(1)}, u32[]{:S(2)}, u32[]{:S(2)}) collective-permute-start(f32[8,512]{1,0:T(8,128)S(1)} %copy.39), channel_id=1, source_target_pairs={{4,0},{0,4},{5,1},{1,5},{6,2},{2,6},{7,3},{3,7},{12,8},{8,12},{13,... | collective-permute-start | bytes 49160 | tf_op jit(solution)/shard_map/ppermute | solution.py:21
  13.3 9.2 %copy-start.6 = (s32[2,1,1,512]{3,2,1,0:T(1,128)S(1)}, s32[2,1,1,512]{3,2,1,0:T(1,128)}, u32[]{:S(2)}) copy-start(s32[2,1,1,512]{3,2,1,0:T(1,128)} %param.16) | copy-start | bytes 12292
  13.3 9.8 %copy-start.7 = (f32[2,1,1,512]{3,2,1,0:T(1,128)S(1)}, f32[2,1,1,512]{3,2,1,0:T(1,128)}, u32[]{:S(2)}) copy-start(f32[2,1,1,512]{3,2,1,0:T(1,128)} %param.15) | copy-start | bytes 12292
  13.3 9.8 %copy-start.8 = (f32[2,1,1,512]{3,2,1,0:T(1,128)S(1)}, f32[2,1,1,512]{3,2,1,0:T(1,128)}, u32[]{:S(2)}) copy-start(f32[2,1,1,512]{3,2,1,0:T(1,128)} %param.14) | copy-start | bytes 12292
  14.4 22.1 %all-to-all-start = ((f32[16,8,1024]{2,1,0:T(8,128)}), f32[16,8,1024]{2,1,0:T(8,128)S(1)}, u32[]{:S(2)}, u32[]{:S(2)}) async-start(f32[16,8,1024]{2,1,0:T(8,128)} %bitcast.105), calls=%async_computation | async-start | bytes 1048576 | tf_op jit(solution)/shard_map/all_to_all | solution.py:269
  36.5 1.4 copy-start.1
  88.8 2.6 %collective-permute-start.2 = (f32[8,512]{1,0:T(8,128)S(1)}, f32[8,512]{1,0:T(8,128)S(1)}, u32[]{:S(2)}, u32[]{:S(2)}) collective-permute-start(f32[8,512]{1,0:T(8,128)S(1)} %reshape.75), channel_id=1, source_target_pairs={{0,4},{4,0},{1,5},{5,1},{2,6},{6,2},{3,7},{7,3},{8,12},{12,8},{9,1... | collective-permute-start | bytes 49160 | tf_op jit(solution)/shard_map/ppermute | solution.py:21
  90.3 2.6 %collective-permute-start.3 = (f32[8,512]{1,0:T(8,128)S(1)}, f32[8,512]{1,0:T(8,128)S(1)}, u32[]{:S(2)}, u32[]{:S(2)}) collective-permute-start(f32[8,512]{1,0:T(8,128)S(1)} %reshape.77), channel_id=1, source_target_pairs={{4,0},{0,4},{5,1},{1,5},{6,2},{2,6},{7,3},{3,7},{12,8},{8,12},{13,... | collective-permute-start | bytes 49160 | tf_op jit(solution)/shard_map/ppermute | solution.py:21
  103.2 21.5 %all-to-all-start.1 = ((f32[16,8,1024]{2,1,0:T(8,128)}), f32[16,8,1024]{2,1,0:T(8,128)S(1)}, u32[]{:S(2)}, u32[]{:S(2)}) async-start(f32[16,8,1024]{2,1,0:T(8,128)} %bitcast.103), calls=%async_computation.1 | async-start | bytes 1048576 | tf_op jit(solution)/shard_map/all_to_all | solution.py:269
  124.7 1.2 copy-start.2
where the time goes:
time: 178 us; the launch traced here: 177 us
  Pallas kernels  94.2 us (53%)
  waiting for transfers between devices  27 us (15%)
  starting transfers between devices  18.5 us (10%)
  local copies, waits for them, and re-layouts  18.2 us (10%)
  other arithmetic  12.9 us (7%)
  matrix products  5.44 us (3%)
    pallas_call x2, Pallas kernels, analysed(): pl.pallas_call(functools.partial(analysis, sizes, count), out_shape=jax.S...  94.2 us
    all_to_all x2, waiting for transfers between devices, shards(): lax.all_to_all(to_slabs(height, slab_count), ('mem', 'grp'), split_axis=0...  23.9 us
    all_to_all x2, starting transfers between devices, shards(): lax.all_to_all(to_slabs(height, slab_count), ('mem', 'grp'), split_axis=0...  15.4 us
    mul x8, other arithmetic, substep(): fluxes = moved * height[..., 1:-1]  7.16 us
    dot_general x8, matrix products, substep(): jnp.einsum('lk,mkc->mlc', coupling, height, precision=lax.Precision.HIGHEST)  5.44 us
    reshape x8, local copies, waits for them, and re-layouts, to_slabs(): return field.reshape(block, slab_count, -1).transpose(1, 0, 2)  5.14 us
    reshape x2, local copies, waits for them, and re-layouts, shards(): members = shaped.transpose(2, 0, 1, 3, 4).reshape(ensemble.shape)  4.64 us
  transfers between devices with their start and end apart: 6, of which 6 were waited for; matrix products, arithmetic and copies ran while one was open for 3% of the time, Pallas kernels for 0%

commit v1 on v0

v1 whole, which is shorter than its diff:
```python
import functools

import jax
import jax.numpy as jnp
from jax import lax
from jax.experimental import pallas as pl
from jax.experimental.pallas import tpu as pltpu
from jax.sharding import PartitionSpec as P

SUBSTEPS = 4
ROOT_STEPS = 8
MESH = pl.DeviceIdType.MESH
LANES = 128
HALO = 2 * SUBSTEPS

time_step = 0.2


def split(value):
    high = value.astype(jnp.bfloat16)
    return high, (value - high.astype(jnp.float32)).astype(jnp.bfloat16)


def split3(value):
    high, rest = value.astype(jnp.bfloat16), None
    rest = value - high.astype(jnp.float32)
    middle = rest.astype(jnp.bfloat16)
    low = (rest - middle.astype(jnp.float32)).astype(jnp.bfloat16)
    return high, middle, low


def one(a, b, across=0):
    dims = (((1,), (across,)), ((), ()))
    return lax.dot_general(a, b, dims, preferred_element_type=jnp.float32)


def product(left, right, across=0):
    left_high, left_low = split(left)
    right_high, right_low = split(right)
    return one(left_high, right_high, across) + (
        one(left_high, right_low, across) + one(left_low, right_high, across)
    )


def iota(shape, axis):
    return lax.broadcasted_iota(jnp.int32, shape, axis)


def program(
    sizes, count, cycles,
    x_ref, coupling_ref, column_ref, level_ref, value_ref, error_ref, live_ref, blend_ref,
    out_ref,
    kron, u_ref, h_ref, p_ref, edge_u, edge_h, edge_p, packed, halo,
    heights, speeds, updated, returned, cells,
    own, column, partial, arrived, peers_blend,
    send_n, recv_n, send_a, recv_a, send_b, recv_b, send_c, recv_c,
    send_h, recv_h, send_u, recv_u, send_e, recv_e,
):
    mem_count, grp_count, hor_count = sizes
    mem = lax.axis_index("mem")
    grp = lax.axis_index("grp")
    hor = lax.axis_index("hor")
    slab_count = mem_count * grp_count
    slab = mem * grp_count + grp
    slab_levels, block, width = x_ref.shape[2:]
    levels = slab_count * slab_levels
    rows = levels * block
    members = slab_count * block

    def grp_peer(step):
        return lax.rem(grp + step, grp_count)

    upper = mem // (mem_count // 2)

    def far_mem(at):
        low = mem_count - 1 - at - (mem + 1 + at) // mem_count
        high = at + (at + mem_count - mem) // mem_count
        return (1 - upper) * low + upper * high

    peers = []
    for at in range(mem_count - 1):
        for step in range(grp_count):
            peers.append((far_mem(at), grp_peer(step)))
    near = [(mem, grp_peer(step)) for step in range(1, grp_count)]

    barrier = pltpu.get_barrier_semaphore()
    right = lax.rem(hor + 1, hor_count)
    left = lax.rem(hor + hor_count - 1, hor_count)
    for one_mem, one_grp in peers + near:
        pl.semaphore_signal(
            barrier, inc=1, device_id={"mem": one_mem, "grp": one_grp}, device_id_type=MESH
        )
    for side in (left, right):
        pl.semaphore_signal(barrier, inc=1, device_id={"hor": side}, device_id_type=MESH)

    def pack(source):
        lane = iota((block, LANES), 1)
        per = LANES // HALO
        for group in range(2 * levels // per):
            low = jnp.zeros((block, LANES), jnp.float32)
            high = jnp.zeros((block, LANES), jnp.float32)
            for at in range(per):
                index = group * per + at
                field, level = index // levels, index % levels
                place = (field, level // slab_levels, level % slab_levels)
                inside = (lane >= at * HALO) & (lane < (at + 1) * HALO)
                first = source[place + (slice(None), slice(0, LANES))]
                last = source[place + (slice(None), slice(width - LANES, width))]
                if at:
                    first = pltpu.roll(first, at * HALO, 1)
                turn = (at * HALO + HALO) % LANES
                if turn:
                    last = pltpu.roll(last, turn, 1)
                low = jnp.where(inside, first, low)
                high = jnp.where(inside, last, high)
            packed[0, group] = low
            packed[1, group] = high

    def send_halo(cycle):
        copies = []
        for side, target in ((0, left), (1, right)):
            copy = pltpu.make_async_remote_copy(
                src_ref=packed.at[side], dst_ref=halo.at[cycle, side],
                send_sem=send_n.at[cycle, side], recv_sem=recv_n.at[cycle, side],
                device_id={"hor": target}, device_id_type=MESH,
            )
            copy.start()
            copies.append(copy)
        return copies

    def unpack(source, cycle):
        lane = iota((block, LANES), 1)
        per = LANES // HALO
        for field, target in ((0, edge_u), (1, edge_h)):
            for level in range(levels):
                index = field * levels + level
                group, at = index // per, index % per
                place = (level // slab_levels, level % slab_levels)
                before = halo[cycle, 1, group]
                after = halo[cycle, 0, group]
                if at:
                    before = pltpu.roll(before, LANES - at * HALO, 1)
                turn = (2 * LANES - HALO - at * HALO) % LANES
                if turn:
                    after = pltpu.roll(after, turn, 1)
                first = source[(field,) + place + (slice(None), slice(0, LANES))]
                last = source[(field,) + place + (slice(None), slice(width - LANES, width))]
                mixed = jnp.where(
                    lane < LANES // 2,
                    pltpu.roll(first, HALO, 1), pltpu.roll(last, LANES - HALO, 1),
                )
                mixed = jnp.where(lane < HALO, before, mixed)
                target[place] = jnp.where(lane >= LANES - HALO, after, mixed)

    def centred(field):
        return (pltpu.roll(field, field.shape[-1] - 1, 1) - pltpu.roll(field, 1, 1)) * 0.5

    def substep(read_u, read_h, write_u, write_h, press):
        span = press.shape[-1]
        for at in range(span // LANES):
            lanes = slice(at * LANES, (at + 1) * LANES)
            high, low = split(read_h(slice(0, slab_count), lanes).reshape(rows, LANES))
            result = one(kron[0], high) + (one(kron[0], low) + one(kron[1], high))
            press[:, :, :, lanes] = result.reshape(slab_count, slab_levels, block, LANES)
        everything = slice(0, span)

        for at in range(slab_count):
            part = slice(at, at + 1)
            size = (slab_levels * block, span)
            velocity = read_u(part, everything).reshape(size)
            height = read_h(part, everything).reshape(size)
            pressure = press[part].reshape(size)
            moved = velocity - time_step * (velocity * centred(velocity) + centred(pressure))
            risen = height - time_step * centred(moved * height)
            write_u[part] = moved.reshape(1, slab_levels, block, span)
            write_h[part] = risen.reshape(1, slab_levels, block, span)

    def reader(ref):
        return lambda part, lanes: ref[part, :, :, lanes]

    def field_reader(ref, field):
        return lambda part, lanes: ref[field, part, :, :, lanes]

    def advance(source, cycle, copies):
        substep(field_reader(source, 0), field_reader(source, 1), u_ref, h_ref, p_ref)

        def again(step, carry):
            substep(reader(u_ref), reader(h_ref), u_ref, h_ref, p_ref)
            return carry

        lax.fori_loop(1, SUBSTEPS, again, 0)
        for copy in copies:
            copy.wait()
        unpack(source, cycle)

        def edge(step, carry):
            substep(reader(edge_u), reader(edge_h), edge_u, edge_h, edge_p)
            return carry

        lax.fori_loop(0, SUBSTEPS, edge, 0)
        lane = iota((block, LANES), 1)
        for strip, whole in ((edge_h, h_ref), (edge_u, u_ref)):
            for at in range(slab_count):
                for level in range(slab_levels):
                    fresh = strip[at, level]
                    first = whole[at, level, :, 0:LANES]
                    last = whole[at, level, :, width - LANES : width]
                    whole[at, level, :, 0:LANES] = jnp.where(
                        lane < HALO, pltpu.roll(fresh, LANES - HALO, 1), first
                    )
                    whole[at, level, :, width - LANES : width] = jnp.where(
                        lane >= LANES - HALO, pltpu.roll(fresh, HALO, 1), last
                    )

    def remote(source, target, send_sem, recv_sem, one_mem, one_grp):
        other = one_mem * grp_count + one_grp
        return pltpu.make_async_remote_copy(
            src_ref=source.at[other], dst_ref=target.at[slab],
            send_sem=send_sem.at[other], recv_sem=recv_sem.at[slab],
            device_id={"mem": one_mem, "grp": one_grp}, device_id_type=MESH,
        )

    def send_all(source, target, send_sem, recv_sem, listed):
        copies = []
        for one_mem, one_grp in listed:
            copy = remote(source, target, send_sem, recv_sem, one_mem, one_grp)
            copy.start()
            copies.append(copy)
        return copies

    def take_all(target, recv_sem):
        for one_mem, one_grp in near + peers:
            other = one_mem * grp_count + one_grp
            pltpu.make_async_remote_copy(
                src_ref=target.at[other], dst_ref=target.at[other],
                send_sem=recv_sem.at[other], recv_sem=recv_sem.at[other],
                device_id={"mem": one_mem, "grp": one_grp}, device_id_type=MESH,
            ).wait_recv()

    def sum_cells(cycle):
        place = level_ref[cycle] * width + column_ref[cycle]
        weight = live_ref[cycle].astype(jnp.float32) / error_ref[cycle]
        pulled = weight * value_ref[cycle]
        parts = split3(weight) + split3(pulled)
        spare = jnp.zeros((16 - len(parts), weight.shape[1]), jnp.bfloat16)
        lhs = jnp.concatenate(parts + (spare,), axis=0)
        total = slab_levels * width

        def chunk(at, carry):
            numbers = iota((LANES, weight.shape[1]), 0) + at * LANES
            hits = jnp.where(numbers == place, 1.0, 0.0).astype(jnp.bfloat16)
            sums = one(lhs, hits, 1)
            cells[0, at] = sums[0:1] + (sums[1:2] + sums[2:3])
            cells[1, at] = sums[3:4] + (sums[4:5] + sums[5:6])
            return carry

        lax.fori_loop(0, total // LANES, chunk, 0)

    def gram():
        per = width // LANES
        total = None
        for level in range(slab_levels):
            flat = heights[:, level].reshape(members, width)
            average = jnp.mean(flat, axis=0, keepdims=True)
            anomalies = flat - average
            weight = jnp.concatenate(
                [cells[0, level * per + at] for at in range(per)], axis=1
            )
            pulled = jnp.concatenate(
                [cells[1, level * per + at] for at in range(per)], axis=1
            )
            pull = pulled - weight * average
            lhs = jnp.concatenate(
                [anomalies * weight, jnp.broadcast_to(pull, (8, width))], axis=0
            )
            here = product(lhs, anomalies, 1)
            total = here if total is None else total + here
        own[...] = total

    lanes = iota((1, blend_ref.shape[1]), 1)

    def share(row, step):
        place = lax.rem(mem + mem_count - step, mem_count) * grp_count + grp
        return jnp.sum(jnp.where(lanes == place, row[0:1], 0.0), axis=1, keepdims=True)

    def blended_for(row):
        total = share(row, 0) * own[...]
        for step in range(1, mem_count):
            total = total + share(row, step) * column[step - 1]
        return total

    def root(total):
        total = total / (count + 1.0)
        square = (members, members)
        identity = (iota(square, 0) == iota(square, 1)).astype(jnp.float32)
        blended = (members - 1.0) * identity + total[:members]
        bvector = total[members:]
        squares = jnp.sum(
            jnp.sum(blended * blended, axis=1, keepdims=True), axis=0, keepdims=True
        )
        frobenius = jnp.sqrt(squares)
        iterate = blended / frobenius
        newton = 1.5 * identity - 0.5 * iterate
        inverse_root = newton
        for step in range(1, ROOT_STEPS):
            iterate = product(newton, iterate)
            newton = 1.5 * identity - 0.5 * product(inverse_root, iterate)
            inverse_root = product(newton, inverse_root)
        spread = inverse_root * (jnp.sqrt(members - 1.0) / jnp.sqrt(frobenius))
        inner = product(bvector, inverse_root)
        mean_weight = product(inner, inverse_root) / frobenius
        return spread + mean_weight[0:1]

    def update(transposed, source, field):
        high, low = split(transposed)
        for level in range(slab_levels):
            flat = source[:, level].reshape(members, width)
            average = jnp.mean(flat, axis=0, keepdims=True)
            flat_high, flat_low = split(flat - average)
            result = average + (
                one(high, flat_high) + (one(high, flat_low) + one(low, flat_high))
            )
            updated[field, :, level] = result.reshape(slab_count, block, width)

    pack(x_ref)
    pl.semaphore_wait(barrier, slab_count - 1 + 2)
    copies = send_halo(0)
    blends = []
    for step in range(1, grp_count):
        copy = pltpu.make_async_remote_copy(
            src_ref=blend_ref, dst_ref=peers_blend.at[step - 1],
            send_sem=send_b.at[step - 1], recv_sem=recv_b.at[step - 1],
            device_id={"grp": grp_peer(step)}, device_id_type=MESH,
        )
        copy.start()
        blends.append(copy)
    spread_rows = jnp.where(
        iota((rows, levels), 0) // block == iota((rows, levels), 1), 1.0, 0.0
    ).astype(jnp.bfloat16)
    same = lax.rem(iota((rows, rows), 0), block) == lax.rem(iota((rows, rows), 1), block)
    for at, part in enumerate(split(coupling_ref[...])):
        tall = one(spread_rows, part).astype(jnp.bfloat16)
        kron[at] = jnp.where(same, one(tall, spread_rows, 1), 0.0).astype(jnp.bfloat16)

    for cycle in range(cycles):
        source = x_ref if cycle == 0 else returned
        if cycle:
            pack(source)
            copies = send_halo(cycle)
        advance(source, cycle, copies)
        outward = send_all(h_ref, heights, send_h.at[cycle], recv_h.at[cycle], peers + near)
        heights[slab] = h_ref[slab]
        speeds[slab] = u_ref[slab]
        sum_cells(cycle)
        take_all(heights, recv_h.at[cycle])
        gram()

        gathers = []
        for step in range(1, mem_count):
            copy = pltpu.make_async_remote_copy(
                src_ref=own, dst_ref=column.at[step - 1],
                send_sem=send_a.at[cycle, step - 1], recv_sem=recv_a.at[cycle, step - 1],
                device_id={"mem": lax.rem(mem + step, mem_count)}, device_id_type=MESH,
            )
            copy.start()
            gathers.append(copy)
        outward = outward + send_all(
            u_ref, speeds, send_u.at[cycle], recv_u.at[cycle], peers
        )
        if cycle == 0:
            for copy in blends:
                copy.wait()
        for copy in gathers:
            copy.wait()
        returns = []
        for step in range(1, grp_count):
            partial[step - 1] = blended_for(peers_blend[step - 1])
            copy = pltpu.make_async_remote_copy(
                src_ref=partial.at[step - 1], dst_ref=arrived.at[step - 1],
                send_sem=send_c.at[cycle, step - 1], recv_sem=recv_c.at[cycle, step - 1],
                device_id={"grp": grp_peer(grp_count - step)}, device_id_type=MESH,
            )
            copy.start()
            returns.append(copy)
        outward = outward + send_all(
            u_ref, speeds, send_u.at[cycle], recv_u.at[cycle], near
        )
        total = blended_for(blend_ref[...])
        for copy in returns:
            copy.wait()
        for step in range(1, grp_count):
            total = total + arrived[step - 1]
        transposed = root(total)
        update(transposed, heights, 1)
        back = send_all(
            updated.at[1], returned.at[1], send_e.at[cycle, 1], recv_e.at[cycle, 1],
            peers + near,
        )
        returned[1, slab] = updated[1, slab]
        take_all(speeds, recv_u.at[cycle])
        update(transposed, speeds, 0)
        back = back + send_all(
            updated.at[0], returned.at[0], send_e.at[cycle, 0], recv_e.at[cycle, 0],
            peers + near,
        )
        returned[0, slab] = updated[0, slab]
        for copy in outward:
            copy.wait_send()
        take_all(returned.at[1], recv_e.at[cycle, 1])
        take_all(returned.at[0], recv_e.at[cycle, 0])
        for copy in back:
            copy.wait_send()
    out_ref[...] = returned[...]


def shards(ensemble, coupling, obs_column, obs_level, obs_value, obs_error, obs_live, partners):
    mem_count = lax.axis_size("mem")
    grp_count = lax.axis_size("grp")
    hor_count = lax.axis_size("hor")
    slab_count = mem_count * grp_count
    own_slab = lax.axis_index("mem") * grp_count + lax.axis_index("grp")
    lanes = max(128, -(-slab_count // 128) * 128)
    slab_numbers = jnp.arange(lanes, dtype=jnp.int32)
    chosen = partners[0, 0]
    count = chosen.shape[0]
    blend_weights = (slab_numbers == own_slab).astype(jnp.float32)
    blend_weights = blend_weights + jnp.sum(
        (slab_numbers[:, None] == chosen[None, :]).astype(jnp.float32), axis=1
    )
    blend = jnp.broadcast_to(blend_weights, (8, lanes))
    block, fields, levels, width = ensemble.shape
    cycles = obs_column.shape[0]
    members = block * slab_count
    slab_levels = levels // slab_count
    x = ensemble.reshape(block, fields, slab_count, slab_levels, width).transpose(1, 2, 3, 0, 4)
    state = (slab_count, slab_levels, block, width)
    strip = (slab_count, slab_levels, block, LANES)
    tall = (members + 8, members)
    rows = levels * block
    groups = 2 * levels * HALO // LANES
    vmem = pl.BlockSpec(memory_space=pltpu.VMEM)
    dma = pltpu.SemaphoreType.DMA
    f32 = jnp.float32
    result = pl.pallas_call(
        functools.partial(program, (mem_count, grp_count, hor_count), count, cycles),
        out_shape=jax.ShapeDtypeStruct((2,) + state, f32),
        in_specs=[vmem] * 8,
        out_specs=vmem,
        scratch_shapes=[
            pltpu.VMEM((2, rows, rows), jnp.bfloat16),
            pltpu.VMEM(state, f32), pltpu.VMEM(state, f32), pltpu.VMEM(state, f32),
            pltpu.VMEM(strip, f32), pltpu.VMEM(strip, f32), pltpu.VMEM(strip, f32),
            pltpu.VMEM((2, groups, block, LANES), f32),
            pltpu.VMEM((cycles, 2, groups, block, LANES), f32),
            pltpu.VMEM(state, f32), pltpu.VMEM(state, f32),
            pltpu.VMEM((2,) + state, f32), pltpu.VMEM((2,) + state, f32),
            pltpu.VMEM((2, slab_levels * width // LANES, 1, LANES), f32),
            pltpu.VMEM(tall, f32),
            pltpu.VMEM((mem_count - 1,) + tall, f32),
            pltpu.VMEM((grp_count - 1,) + tall, f32),
            pltpu.VMEM((grp_count - 1,) + tall, f32),
            pltpu.VMEM((grp_count - 1,) + blend.shape, f32),
            dma((cycles, 2)), dma((cycles, 2)),
            dma((cycles, mem_count - 1)), dma((cycles, mem_count - 1)),
            dma((grp_count - 1,)), dma((grp_count - 1,)),
            dma((cycles, grp_count - 1)), dma((cycles, grp_count - 1)),
            dma((cycles, slab_count)), dma((cycles, slab_count)),
            dma((cycles, slab_count)), dma((cycles, slab_count)),
            dma((cycles, 2, slab_count)), dma((cycles, 2, slab_count)),
        ],
        compiler_params=pltpu.CompilerParams(collective_id=0, has_side_effects=True),
    )(
        x, coupling, obs_column[:, 0], obs_level[:, 0], obs_value[:, 0], obs_error[:, 0],
        obs_live[:, 0], blend,
    )
    return result.transpose(3, 0, 1, 2, 4).reshape(ensemble.shape)


def solution(mesh):
    in_specs = (
        P(("mem", "grp"), None, None, "hor"),
        P(),
        P(None, ("mem", "grp"), "hor", None),
        P(None, ("mem", "grp"), "hor", None),
        P(None, ("mem", "grp"), "hor", None),
        P(None, ("mem", "grp"), "hor", None),
        P(None, ("mem", "grp"), "hor", None),
        P(("mem", "grp"), "hor", None),
    )
    out_specs = P(("mem", "grp"), None, None, "hor")
    return jax.shard_map(shards, mesh=mesh, in_specs=in_specs, out_specs=out_specs, check_vma=False)
```

time: 178 us -> 149 us (0.84)
  Pallas kernels: 94.2 us -> 141 us
  waiting for transfers between devices: 27 us -> 0 us
  starting transfers between devices: 18.5 us -> 0 us
  other arithmetic: 12.9 us -> 0.09 us
  local copies, waits for them, and re-layouts: 18.2 us -> 6.86 us
  matrix products: 5.44 us -> 0 us
    pallas_call x2 -> x1, Pallas kernels: 94.2 us -> 141 us  [shards(): pl.pallas_call(functools.partial(program, (mem_count, grp_count, hor_coun...]
    all_to_all x2 -> x0, waiting for transfers between devices: 23.9 us -> none  [shards(): lax.all_to_all(to_slabs(height, slab_count), ('mem', 'grp'), split_axis=0...]
    all_to_all x2 -> x0, starting transfers between devices: 15.4 us -> none  [shards(): lax.all_to_all(to_slabs(height, slab_count), ('mem', 'grp'), split_axis=0...]
    reshape x24 -> x1, local copies, waits for them, and re-layouts: 11.6 us -> 2.81 us  [shards(): return result.transpose(3, 0, 1, 2, 4).reshape(ensemble.shape)]
    mul x8 -> x0, other arithmetic: 7.16 us -> none  [substep(): fluxes = moved * height[..., 1:-1]]
    dot_general x8 -> x0, matrix products: 5.44 us -> none  [substep(): jnp.einsum('lk,mkc->mlc', coupling, height, precision=lax.Precision.HIGHEST)]
    unnamed x20 -> x3, local copies, waits for them, and re-layouts: 0.05 us -> 3.46 us
    sub x8 -> x0, other arithmetic: 3.14 us -> none  [substep(): height_new = height[..., 2:-2] - time_step * centred(fluxes)]
  transfers between devices with their start and end apart: 6 -> 0, of which waited for: 6 -> 0; matrix products, arithmetic and copies ran while one was open for 3% -> 0% of each run, Pallas kernels for 0% -> 0%
where the time goes in v1:
time: 149 us; the launch traced here: 148 us
  Pallas kernels  141 us (95%)
  local copies, waits for them, and re-layouts  6.86 us (5%)
    pallas_call x1, Pallas kernels, shards(): pl.pallas_call(functools.partial(program, (mem_count, grp_count, hor_coun...  141 us
    unnamed x3, local copies, waits for them, and re-layouts  3.46 us

profile of v1, /device:TPU:11, one launch (start us, length us, event | category | flops | bytes accessed | tf_op | source)
XLA Modules:
  0.0 147.9 jit_solution(3777831485416450815)
XLA Ops:
  0.0 0.0 copy-start
  0.0 0.7 copy-done
  0.7 0.1 fusion
  0.7 0.6 broadcast_in_dim.4.blend_ref
  1.3 2.8 %copy.11 = f32[8,2,32,512]{3,0,2,1:T(8,128)} copy(f32[8,2,32,512]{3,2,1,0:T(8,128)} %param.8) | data formatting | bytes 2097152 | tf_op args[0]
  4.1 140.9 %shard_map.82 = f32[2,16,2,8,512]{4,3,2,1,0:T(8,128)} custom-call(f32[2,16,2,8,512]{4,3,2,1,0:T(8,128)} %bitcast.13, f32[32,32]{1,0:T(8,128)} %coupling_ref.1, s32[2,1,512]{2,1,0:T(1,128)} %bitcast.14, s32[2,1,512]{2,1,0:T(1,128)} %bitcast.15, f32[2,1,512]{2,1,0:T(1,128)} %bitcast.16, f32[2,1,512]{2,1,0:T(1,128)} %bitcast.17, s32[2,1,512]{2,1,0:T(1,128)} %bitcast.18, ...), custom_call_target="tpu_custom_call" | custom-call | tf_op jit(solution)/shard_map/pallas_call | solution.py:444
  145.1 2.8 %copy.12 = f32[8,2,32,512]{3,2,1,0:T(8,128)} copy(f32[8,2,32,512]{3,0,2,1:T(8,128)} %bitcast.12) | data formatting | bytes 2097152 | tf_op jit(solution)/shard_map/reshape | solution.py:476
  (1 shorter events, 0.0 us)
Async XLA Ops:
  0.0 0.7 copy-start

commit v2 on v1

--- a/solution.py
+++ b/solution.py
@@ -51,47 +51,68 @@
     x_ref, coupling_ref, column_ref, level_ref, value_ref, error_ref, live_ref, blend_ref,
     out_ref,
     kron, u_ref, h_ref, p_ref, edge_u, edge_h, edge_p, packed, halo,
-    heights, speeds, updated, returned, cells,
-    own, column, partial, arrived, peers_blend,
-    send_n, recv_n, send_a, recv_a, send_b, recv_b, send_c, recv_c,
-    send_h, recv_h, send_u, recv_u, send_e, recv_e,
+    heights, speeds, updated, returned, final, relayed, cells, bundle, notes,
+    own, column, partial, arrived, blends,
+    send_n, recv_n, send_o, recv_o, send_a, recv_a, send_b, recv_b, send_c, recv_c,
+    send_h, recv_h, send_u, recv_u, send_e, recv_e, send_f, recv_f,
+    send_r, recv_r, send_g,
 ):
     mem_count, grp_count, hor_count = sizes
     mem = lax.axis_index("mem")
     grp = lax.axis_index("grp")
     hor = lax.axis_index("hor")
     slab_count = mem_count * grp_count
-    slab = mem * grp_count + grp
     slab_levels, block, width = x_ref.shape[2:]
     levels = slab_count * slab_levels
     rows = levels * block
     members = slab_count * block
 
-    def grp_peer(step):
-        return lax.rem(grp + step, grp_count)
-
-    upper = mem // (mem_count // 2)
-
-    def far_mem(at):
-        low = mem_count - 1 - at - (mem + 1 + at) // mem_count
-        high = at + (at + mem_count - mem) // mem_count
-        return (1 - upper) * low + upper * high
-
-    peers = []
-    for at in range(mem_count - 1):
-        for step in range(grp_count):
-            peers.append((far_mem(at), grp_peer(step)))
-    near = [(mem, grp_peer(step)) for step in range(1, grp_count)]
+    depth = mem_count // 2
+    pairs = hor_count // 2
+    pair = hor // 2
+    side = lax.rem(hor, 2)
+    half = mem // depth
+    deep = lax.rem(mem, depth)
+    away = half + side - 2 * half * side
+    line = side * depth + deep
+    slab = line * grp_count + grp
+    first_block = mem * grp_count + grp
+
+    def turned(at, step, size):
+        return lax.rem(at + step, size)
+
+    def spot(in_half, step_side, step_deep, step_grp):
+        to_side = turned(side, step_side, 2)
+        to_deep = turned(deep, step_deep, depth)
+        to_grp = turned(grp, step_grp, grp_count)
+        device = {"mem": in_half * depth + to_deep, "hor": 2 * pair + to_side, "grp": to_grp}
+        return device, (to_side * depth + to_deep) * grp_count + to_grp
+
+    steps = [
+        (one_side, one_deep, one_grp)
+        for one_side in range(2) for one_deep in range(depth) for one_grp in range(grp_count)
+    ]
+    cube = [spot(half, *step) for step in steps[:0:-1]]
+    across = [(at, spot(1 - half, 0, *step[1:])) for at, step in enumerate(steps[: len(steps) // 2])]
+
+    right = ({"hor": turned(hor, 1, hor_count)},
+             {"mem": turned(mem, depth, mem_count),
+              "hor": 2 * turned(pair, half, pairs) + side})
+    left = ({"hor": turned(hor, hor_count - 1, hor_count)},
+            {"mem": turned(mem, depth, mem_count),
+             "hor": 2 * turned(pair, half + pairs - 1, pairs) + side})
 
     barrier = pltpu.get_barrier_semaphore()
-    right = lax.rem(hor + 1, hor_count)
-    left = lax.rem(hor + hor_count - 1, hor_count)
-    for one_mem, one_grp in peers + near:
-        pl.semaphore_signal(
-            barrier, inc=1, device_id={"mem": one_mem, "grp": one_grp}, device_id_type=MESH
+    for device, _ in cube + [spot(1 - half, *step) for step in steps]:
+        pl.semaphore_signal(barrier, inc=1, device_id=device, device_id_type=MESH)
+    for device in left + right:
+        pl.semaphore_signal(barrier, inc=1, device_id=device, device_id_type=MESH)
+
+    def remote(source, target, send_sem, recv_sem, device):
+        return pltpu.make_async_remote_copy(
+            src_ref=source, dst_ref=target, send_sem=send_sem, recv_sem=recv_sem,
+            device_id=device, device_id_type=MESH,
         )
-    for side in (left, right):
-        pl.semaphore_signal(barrier, inc=1, device_id={"hor": side}, device_id_type=MESH)
 
     def pack(source):
         lane = iota((block, LANES), 1)
@@ -118,11 +139,10 @@
 
     def send_halo(cycle):
         copies = []
-        for side, target in ((0, left), (1, right)):
-            copy = pltpu.make_async_remote_copy(
-                src_ref=packed.at[side], dst_ref=halo.at[cycle, side],
-                send_sem=send_n.at[cycle, side], recv_sem=recv_n.at[cycle, side],
-                device_id={"hor": target}, device_id_type=MESH,
+        for at, target in ((0, left[cycle > 0]), (1, right[cycle > 0])):
+            copy = remote(
+                packed.at[at], halo.at[cycle, at],
+                send_n.at[cycle, at], recv_n.at[cycle, at], target,
             )
             copy.start()
             copies.append(copy)
@@ -212,35 +232,150 @@
                         lane >= LANES - HALO, pltpu.roll(fresh, HALO, 1), last
                     )
 
-    def remote(source, target, send_sem, recv_sem, one_mem, one_grp):
-        other = one_mem * grp_count + one_grp
-        return pltpu.make_async_remote_copy(
-            src_ref=source.at[other], dst_ref=target.at[slab],
-            send_sem=send_sem.at[other], recv_sem=recv_sem.at[slab],
-            device_id={"mem": one_mem, "grp": one_grp}, device_id_type=MESH,
-        )
-
-    def send_all(source, target, send_sem, recv_sem, listed):
+    def arrive(target, recv_sem, other):
+        remote(
+            target.at[other], target.at[other], recv_sem.at[other], recv_sem.at[other], {"hor": hor}
+        ).wait_recv()
+
+    def cube_send(source, target, send_sem, recv_sem):
         copies = []
-        for one_mem, one_grp in listed:
-            copy = remote(source, target, send_sem, recv_sem, one_mem, one_grp)
+        for device, other in cube:
+            copy = remote(
+                source.at[other], target.at[slab], send_sem.at[other], recv_sem.at[slab], device
+            )
             copy.start()
             copies.append(copy)
         return copies
 
-    def take_all(target, recv_sem):
-        for one_mem, one_grp in near + peers:
-            other = one_mem * grp_count + one_grp
-            pltpu.make_async_remote_copy(
-                src_ref=target.at[other], dst_ref=target.at[other],
-                send_sem=recv_sem.at[other], recv_sem=recv_sem.at[other],
-                device_id={"mem": one_mem, "grp": one_grp}, device_id_type=MESH,
-            ).wait_recv()
+    def cube_take(target, recv_sem):
+        for _, other in cube:
+            arrive(target, recv_sem, other)
+
+    def relay_copy(field, source, at, other):
+        return remote(
+            source.at[other], relayed.at[field, at], send_r.at[field, at], recv_r.at[field, at],
+            {"hor": 2 * pair + 1 - side},
+        )
+
+    def inward_relay(field, source):
+        @pl.when(away == 1)
+        def _():
+            for at, step in enumerate(steps[: len(steps) // 2]):
+                relay_copy(field, source, at, spot(half, 1, *step[1:])[1]).start()
+
+    def inward_copies(spots, source, target, send_sem, recv_sem):
+        return [
+            remote(
+                source.at[other], target.at[first_block],
+                send_sem.at[other], recv_sem.at[first_block], device,
+            )
+            for device, other in spots
+        ]
+
+    straight = [there for _, there in across]
+
+    def forward_copy(field, target, recv_sem, at, device):
+        return remote(
+            relayed.at[field, at], target.at[first_block],
+            send_g.at[field, at], recv_sem.at[first_block], device,
+        )
+
+    def inward_send(field, source, target, send_sem, recv_sem):
+        @pl.when(away == 1)
+        def _():
+            for copy in inward_copies(straight, source, target, send_sem, recv_sem):
+                copy.start()
+
+        @pl.when(away == 0)
+        def _():
+            for copy in inward_copies(cube, source, target, send_sem, recv_sem):
+                copy.start()
+            for at, (device, other) in across:
+                relay_copy(field, source, at, other).wait_recv()
+                forward_copy(field, target, recv_sem, at, device).start()
+
+    def inward_drain(field, source, target, send_sem, recv_sem):
+        @pl.when(away == 1)
+        def _():
+            for copy in inward_copies(straight, source, target, send_sem, recv_sem):
+                copy.wait_send()
+            for at, step in enumerate(steps[: len(steps) // 2]):
+                relay_copy(field, source, at, spot(half, 1, *step[1:])[1]).wait_send()
+
+        @pl.when(away == 0)
+        def _():
+            for copy in inward_copies(cube, source, target, send_sem, recv_sem):
+                copy.wait_send()
+            for at, (device, other) in across:
+                forward_copy(field, target, recv_sem, at, device).wait_send()
+
+    def inward_take(target, recv_sem):
+        for step_mem in range(mem_count):
+            for step_grp in range(grp_count):
+                other = turned(mem, step_mem, mem_count) * grp_count + turned(grp, step_grp, grp_count)
+                if step_mem + step_grp:
+                    arrive(target, recv_sem, other)
+                else:
+                    @pl.when(away == 1)
+                    def _():
+                        arrive(target, recv_sem, other)
+
+    def outward_copies(field):
+        copies = []
+        for step_mem in range(mem_count):
+            for step_grp in range(grp_count):
+                to_mem = turned(mem, step_mem, mem_count)
+                to_grp = turned(grp, step_grp, grp_count)
+                other = to_mem * grp_count + to_grp
+                copies.append(remote(
+                    updated.at[field, other], final.at[field, slab],
+                    send_f.at[field, other], recv_f.at[field, slab],
+                    {"mem": to_mem, "hor": 2 * pair + half, "grp": to_grp},
+                ))
+        return copies
+
+    def outward_send(field):
+        copies = outward_copies(field)
+
+        @pl.when(away == 1)
+        def _():
+            copies[0].start()
+
+        for copy in copies[1:]:
+            copy.start()
+
+        @pl.when(away == 0)
+        def _():
+            final[field, slab] = updated[field, slab]
+
+    def outward_finish(field):
+        for at in range(slab_count):
+            other = turned(slab, at, slab_count)
+            if at:
+                arrive(final.at[field], recv_f.at[field], other)
+            else:
+                @pl.when(away == 1)
+                def _():
+                    arrive(final.at[field], recv_f.at[field], other)
+        copies = outward_copies(field)
+
+        @pl.when(away == 1)
+        def _():
+            copies[0].wait_send()
+
+        for copy in copies[1:]:
+            copy.wait_send()
+
+    def bundle_copy():
+        return remote(
+            bundle, notes, send_o.at[0], recv_o.at[0],
+            {"mem": turned(mem, depth, mem_count), "hor": 2 * pair + 1 - side},
+        )
 
     def sum_cells(cycle):
-        place = level_ref[cycle] * width + column_ref[cycle]
-        weight = live_ref[cycle].astype(jnp.float32) / error_ref[cycle]
-        pulled = weight * value_ref[cycle]
+        place = notes[cycle, 0:1].astype(jnp.int32)
+        weight = notes[cycle, 1:2]
+        pulled = notes[cycle, 2:3]
         parts = split3(weight) + split3(pulled)
         spare = jnp.zeros((16 - len(parts), weight.shape[1]), jnp.bfloat16)
         lhs = jnp.concatenate(parts + (spare,), axis=0)
@@ -280,7 +415,7 @@
     lanes = iota((1, blend_ref.shape[1]), 1)
 
     def share(row, step):
-        place = lax.rem(mem + mem_count - step, mem_count) * grp_count + grp
+        place = turned(line, mem_count - step, mem_count) * grp_count + grp
         return jnp.sum(jnp.where(lanes == place, row[0:1], 0.0), axis=1, keepdims=True)
 
     def blended_for(row):
@@ -323,17 +458,24 @@
             updated[field, :, level] = result.reshape(slab_count, block, width)
 
     pack(x_ref)
-    pl.semaphore_wait(barrier, slab_count - 1 + 2)
+    for cycle in range(cycles):
+        weight = live_ref[cycle].astype(jnp.float32) / error_ref[cycle]
+        place = level_ref[cycle] * width + column_ref[cycle]
+        bundle[cycle, 0:1] = place.astype(jnp.float32)
+        bundle[cycle, 1:2] = weight
+        bundle[cycle, 2:3] = weight * value_ref[cycle]
+    bundle[cycles, :, 0 : blend_ref.shape[1]] = blend_ref[...]
+    pl.semaphore_wait(barrier, 2 * slab_count - 1 + 4)
     copies = send_halo(0)
-    blends = []
-    for step in range(1, grp_count):
-        copy = pltpu.make_async_remote_copy(
-            src_ref=blend_ref, dst_ref=peers_blend.at[step - 1],
-            send_sem=send_b.at[step - 1], recv_sem=recv_b.at[step - 1],
-            device_id={"grp": grp_peer(step)}, device_id_type=MESH,
-        )
-        copy.start()
-        blends.append(copy)
+
+    @pl.when(away == 1)
+    def _():
+        bundle_copy().start()
+
+    @pl.when(away == 0)
+    def _():
+        notes[...] = bundle[...]
+
     spread_rows = jnp.where(
         iota((rows, levels), 0) // block == iota((rows, levels), 1), 1.0, 0.0
     ).astype(jnp.bfloat16)
@@ -342,75 +484,110 @@
         tall = one(spread_rows, part).astype(jnp.bfloat16)
         kron[at] = jnp.where(same, one(tall, spread_rows, 1), 0.0).astype(jnp.bfloat16)
 
+    blend_copies = []
     for cycle in range(cycles):
         source = x_ref if cycle == 0 else returned
         if cycle:
             pack(source)
             copies = send_halo(cycle)
         advance(source, cycle, copies)
-        outward = send_all(h_ref, heights, send_h.at[cycle], recv_h.at[cycle], peers + near)
-        heights[slab] = h_ref[slab]
-        speeds[slab] = u_ref[slab]
+        heights_now = (h_ref, heights, send_h.at[cycle], recv_h.at[cycle])
+        speeds_now = (u_ref, speeds, send_u.at[cycle], recv_u.at[cycle])
+        drains = []
+        if cycle == 0:
+            inward_relay(1, h_ref)
+            inward_send(1, *heights_now)
+            inward_relay(0, u_ref)
+
+            @pl.when(away == 1)
+            def _():
+                bundle_copy().wait()
+
+            @pl.when(away == 0)
+            def _():
+                heights[slab] = h_ref[slab]
+                speeds[slab] = u_ref[slab]
+
+            blends[0] = notes[cycles, 0:8, 0 : blend_ref.shape[1]]
+            for step in range(1, grp_count):
+                copy = remote(
+                    blends.at[0], blends.at[step], send_b.at[step], recv_b.at[step],
+                    {"grp": turned(grp, step, grp_count)},
+                )
+                copy.start()
+                blend_copies.append(copy)
+        else:
+            drains = cube_send(*heights_now)
+            heights[slab] = h_ref[slab]
+            speeds[slab] = u_ref[slab]
         sum_cells(cycle)
-        take_all(heights, recv_h.at[cycle])
+        if cycle == 0:
+            inward_take(heights, recv_h.at[cycle])
+        else:
+            cube_take(heights, recv_h.at[cycle])
         gram()
 
         gathers = []
         for step in range(1, mem_count):
-            copy = pltpu.make_async_remote_copy(
-                src_ref=own, dst_ref=column.at[step - 1],
-                send_sem=send_a.at[cycle, step - 1], recv_sem=recv_a.at[cycle, step - 1],
-                device_id={"mem": lax.rem(mem + step, mem_count)}, device_id_type=MESH,
+            to_line = turned(line, step, mem_count)
+            copy = remote(
+                own, column.at[step - 1], send_a.at[cycle, step - 1], recv_a.at[cycle, step - 1],
+                {"mem": half * depth + lax.rem(to_line, depth), "hor": 2 * pair + to_line // depth},
             )
             copy.start()
             gathers.append(copy)
-        outward = outward + send_all(
-            u_ref, speeds, send_u.at[cycle], recv_u.at[cycle], peers
-        )
         if cycle == 0:
-            for copy in blends:
-                copy.wait()
+            inward_send(0, *speeds_now)
+        else:
+            drains = drains + cube_send(*speeds_now)
+        for copy in blend_copies:
+            copy.wait()
+        blend_copies = []
         for copy in gathers:
             copy.wait()
         returns = []
         for step in range(1, grp_count):
-            partial[step - 1] = blended_for(peers_blend[step - 1])
-            copy = pltpu.make_async_remote_copy(
-                src_ref=partial.at[step - 1], dst_ref=arrived.at[step - 1],
-                send_sem=send_c.at[cycle, step - 1], recv_sem=recv_c.at[cycle, step - 1],
-                device_id={"grp": grp_peer(grp_count - step)}, device_id_type=MESH,
+            partial[step - 1] = blended_for(blends[step])
+            copy = remote(
+                partial.at[step - 1], arrived.at[step - 1],
+                send_c.at[cycle, step - 1], recv_c.at[cycle, step - 1],
+                {"grp": turned(grp, grp_count - step, grp_count)},
             )
             copy.start()
             returns.append(copy)
-        outward = outward + send_all(
-            u_ref, speeds, send_u.at[cycle], recv_u.at[cycle], near
-        )
-        total = blended_for(blend_ref[...])
+        total = blended_for(blends[0])
         for copy in returns:
             copy.wait()
         for step in range(1, grp_count):
             total = total + arrived[step - 1]
         transposed = root(total)
-        update(transposed, heights, 1)
-        back = send_all(
-            updated.at[1], returned.at[1], send_e.at[cycle, 1], recv_e.at[cycle, 1],
-            peers + near,
-        )
-        returned[1, slab] = updated[1, slab]
-        take_all(speeds, recv_u.at[cycle])
-        update(transposed, speeds, 0)
-        back = back + send_all(
-            updated.at[0], returned.at[0], send_e.at[cycle, 0], recv_e.at[cycle, 0],
-            peers + near,
-        )
-        returned[0, slab] = updated[0, slab]
-        for copy in outward:
+        last = cycle == cycles - 1
+        for field, patch in ((1, heights), (0, speeds)):
+            if field == 0:
+                if cycle == 0:
+                    inward_take(speeds, recv_u.at[cycle])
+                else:
+                    cube_take(speeds, recv_u.at[cycle])
+            update(transposed, patch, field)
+            if last:
+                outward_send(field)
+            else:
+                drains = drains + cube_send(
+                    updated.at[field], returned.at[field],
+                    send_e.at[cycle, field], recv_e.at[cycle, field],
+                )
+                returned[field, slab] = updated[field, slab]
+        if not last:
+            for field in (1, 0):
+                cube_take(returned.at[field], recv_e.at[cycle, field])
+        for copy in drains:
             copy.wait_send()
-        take_all(returned.at[1], recv_e.at[cycle, 1])
-        take_all(returned.at[0], recv_e.at[cycle, 0])
-        for copy in back:
-            copy.wait_send()
-    out_ref[...] = returned[...]
+        if cycle == 0:
+            inward_drain(1, *heights_now)
+            inward_drain(0, *speeds_now)
+    for field in (1, 0):
+        outward_finish(field)
+    out_ref[...] = final[...]
 
 
 def shards(ensemble, coupling, obs_column, obs_level, obs_value, obs_error, obs_live, partners):
@@ -438,6 +615,7 @@
     tall = (members + 8, members)
     rows = levels * block
     groups = 2 * levels * HALO // LANES
+    slots = max(obs_column.shape[-1], lanes)
     vmem = pl.BlockSpec(memory_space=pltpu.VMEM)
     dma = pltpu.SemaphoreType.DMA
     f32 = jnp.float32
@@ -454,19 +632,25 @@
             pltpu.VMEM((cycles, 2, groups, block, LANES), f32),
             pltpu.VMEM(state, f32), pltpu.VMEM(state, f32),
             pltpu.VMEM((2,) + state, f32), pltpu.VMEM((2,) + state, f32),
+            pltpu.VMEM((2,) + state, f32),
+            pltpu.VMEM((2, slab_count // 2) + state[1:], f32),
             pltpu.VMEM((2, slab_levels * width // LANES, 1, LANES), f32),
+            pltpu.VMEM((cycles + 1, 8, slots), f32), pltpu.VMEM((cycles + 1, 8, slots), f32),
             pltpu.VMEM(tall, f32),
             pltpu.VMEM((mem_count - 1,) + tall, f32),
             pltpu.VMEM((grp_count - 1,) + tall, f32),
             pltpu.VMEM((grp_count - 1,) + tall, f32),
-            pltpu.VMEM((grp_count - 1,) + blend.shape, f32),
+            pltpu.VMEM((grp_count,) + blend.shape, f32),
             dma((cycles, 2)), dma((cycles, 2)),
+            dma((1,)), dma((1,)),
             dma((cycles, mem_count - 1)), dma((cycles, mem_count - 1)),
-            dma((grp_count - 1,)), dma((grp_count - 1,)),
+            dma((grp_count,)), dma((grp_count,)),
             dma((cycles, grp_count - 1)), dma((cycles, grp_count - 1)),
             dma((cycles, slab_count)), dma((cycles, slab_count)),
             dma((cycles, slab_count)), dma((cycles, slab_count)),
             dma((cycles, 2, slab_count)), dma((cycles, 2, slab_count)),
+            dma((2, slab_count)), dma((2, slab_count)),
+            dma((2, slab_count // 2)), dma((2, slab_count // 2)), dma((2, slab_count // 2)),
         ],
         compiler_params=pltpu.CompilerParams(collective_id=0, has_side_effects=True),
     )(

time: 149 us -> 127 us (0.85)
  Pallas kernels: 141 us -> 119 us
    pallas_call x1, Pallas kernels: 141 us -> 119 us  [shards(): pl.pallas_call(functools.partial(program, (mem_count, grp_count, hor_coun...]
where the time goes in v2:
time: 127 us; the launch traced here: 126 us
  Pallas kernels  119 us (94%)
  local copies, waits for them, and re-layouts  6.86 us (5%)
    pallas_call x1, Pallas kernels, shards(): pl.pallas_call(functools.partial(program, (mem_count, grp_count, hor_coun...  119 us
    unnamed x3, local copies, waits for them, and re-layouts  3.46 us
    reshape x1, local copies, waits for them, and re-layouts, shards(): return result.transpose(3, 0, 1, 2, 4).reshape(ensemble.shape)  2.81 us

profile of v2, /device:TPU:11, one launch (start us, length us, event | category | flops | bytes accessed | tf_op | source)
XLA Modules:
  0.0 126.3 jit_solution(2730168752271946870)
XLA Ops:
  0.0 0.0 copy-start
  0.0 0.7 copy-done
  0.7 0.1 fusion
  0.7 0.6 broadcast_in_dim.4.blend_ref
  1.3 2.8 %copy.11 = f32[8,2,32,512]{3,0,2,1:T(8,128)} copy(f32[8,2,32,512]{3,2,1,0:T(8,128)} %param.8) | data formatting | bytes 2097152 | tf_op args[0]
  4.1 119.4 %shard_map.82 = f32[2,16,2,8,512]{4,3,2,1,0:T(8,128)} custom-call(f32[2,16,2,8,512]{4,3,2,1,0:T(8,128)} %bitcast.13, f32[32,32]{1,0:T(8,128)} %coupling_ref.1, s32[2,1,512]{2,1,0:T(1,128)} %bitcast.14, s32[2,1,512]{2,1,0:T(1,128)} %bitcast.15, f32[2,1,512]{2,1,0:T(1,128)} %bitcast.16, f32[2,1,512]{2,1,0:T(1,128)} %bitcast.17, s32[2,1,512]{2,1,0:T(1,128)} %bitcast.18, ...), custom_call_target="tpu_custom_call" | custom-call | tf_op jit(solution)/shard_map/pallas_call | solution.py:622
  123.5 2.8 %copy.12 = f32[8,2,32,512]{3,2,1,0:T(8,128)} copy(f32[8,2,32,512]{3,0,2,1:T(8,128)} %bitcast.12) | data formatting | bytes 2097152 | tf_op jit(solution)/shard_map/reshape | solution.py:660
  (1 shorter events, 0.0 us)
Async XLA Ops:
  0.0 0.7 copy-start

commit v3 on v2

--- a/solution.py
+++ b/solution.py
@@ -48,9 +48,9 @@
 
 def program(
     sizes, count, cycles,
-    x_ref, coupling_ref, column_ref, level_ref, value_ref, error_ref, live_ref, blend_ref,
+    given_ref, coupling_ref, column_ref, level_ref, value_ref, error_ref, live_ref, chosen_ref,
     out_ref,
-    kron, u_ref, h_ref, p_ref, edge_u, edge_h, edge_p, packed, halo,
+    x_ref, kron, u_ref, h_ref, p_ref, edge_u, edge_h, edge_p, packed, halo,
     heights, speeds, updated, returned, final, relayed, cells, bundle, notes,
     own, column, partial, arrived, blends,
     send_n, recv_n, send_o, recv_o, send_a, recv_a, send_b, recv_b, send_c, recv_c,
@@ -63,6 +63,7 @@
     hor = lax.axis_index("hor")
     slab_count = mem_count * grp_count
     slab_levels, block, width = x_ref.shape[2:]
+    lane_count = blends.shape[2]
     levels = slab_count * slab_levels
     rows = levels * block
     members = slab_count * block
@@ -201,14 +202,18 @@
     def field_reader(ref, field):
         return lambda part, lanes: ref[field, part, :, :, lanes]
 
-    def advance(source, cycle, copies):
+    def advance(source, cycle, greet):
         substep(field_reader(source, 0), field_reader(source, 1), u_ref, h_ref, p_ref)
 
         def again(step, carry):
             substep(reader(u_ref), reader(h_ref), u_ref, h_ref, p_ref)
             return carry
 
-        lax.fori_loop(1, SUBSTEPS, again, 0)
+        ahead = SUBSTEPS // 2 if cycle == 0 else 1
+        if ahead > 1:
+            lax.fori_loop(1, ahead, again, 0)
+        copies = greet()
+        lax.fori_loop(ahead, SUBSTEPS, again, 0)
         for copy in copies:
             copy.wait()
         unpack(source, cycle)
@@ -410,9 +415,30 @@
             )
             here = product(lhs, anomalies, 1)
             total = here if total is None else total + here
-        own[...] = total
-
-    lanes = iota((1, blend_ref.shape[1]), 1)
+        short = members // 2
+        row, lane = iota((short, members), 0), iota((short, members), 1)
+        upper = total[:short]
+        own[:short] = jnp.where(
+            lane - short > row, pltpu.roll(upper, short, 1), total[short:members]
+        )
+        diagonal = jnp.sum(jnp.where(lane == row, upper, 0.0), axis=0, keepdims=True)
+        own[short:] = jnp.where(
+            iota((8, members), 0) == 0, total[members:], jnp.broadcast_to(diagonal, (8, members))
+        )
+
+    def unfold(total):
+        short = members // 2
+        row, lane = iota((short, members), 0), iota((short, members), 1)
+        lower = total[:short]
+        turned_over = jnp.transpose(jnp.concatenate([lower, lower], axis=0))
+        first, second = turned_over[:short], turned_over[short:]
+        inside = jnp.where(lane < row, second, total[short + 1 : short + 2])
+        inside = jnp.where(lane > row, pltpu.roll(lower, short, 1), inside)
+        top = jnp.where(lane >= short, first, inside)
+        bottom = jnp.where(lane - short > row, second, lower)
+        return jnp.concatenate([top, bottom], axis=0), total[short : short + 1]
+
+    lanes = iota((1, lane_count), 1)
 
     def share(row, step):
         place = turned(line, mem_count - step, mem_count) * grp_count + grp
@@ -428,8 +454,9 @@
         total = total / (count + 1.0)
         square = (members, members)
         identity = (iota(square, 0) == iota(square, 1)).astype(jnp.float32)
-        blended = (members - 1.0) * identity + total[:members]
-        bvector = total[members:]
+        whole, bvector = unfold(total)
+        blended = (members - 1.0) * identity + whole
+        bvector = jnp.broadcast_to(bvector, (8, members))
         squares = jnp.sum(
             jnp.sum(blended * blended, axis=1, keepdims=True), axis=0, keepdims=True
         )
@@ -457,6 +484,13 @@
             )
             updated[field, :, level] = result.reshape(slab_count, block, width)
 
+    for field in range(2):
+        for at in range(0, levels, 8):
+            part = given_ref[:, field, at : at + 8]
+            part = jnp.swapaxes(part, 0, 1)
+            x_ref[field, at // slab_levels : (at + 8) // slab_levels] = part.reshape(
+                8 // slab_levels, slab_levels, block, width
+            )
     pack(x_ref)
     for cycle in range(cycles):
         weight = live_ref[cycle].astype(jnp.float32) / error_ref[cycle]
@@ -464,18 +498,11 @@
         bundle[cycle, 0:1] = place.astype(jnp.float32)
         bundle[cycle, 1:2] = weight
         bundle[cycle, 2:3] = weight * value_ref[cycle]
-    bundle[cycles, :, 0 : blend_ref.shape[1]] = blend_ref[...]
-    pl.semaphore_wait(barrier, 2 * slab_count - 1 + 4)
-    copies = send_halo(0)
-
-    @pl.when(away == 1)
-    def _():
-        bundle_copy().start()
-
-    @pl.when(away == 0)
-    def _():
-        notes[...] = bundle[...]
-
+    numbers = iota((8, lane_count), 1)
+    blend = jnp.where(numbers == first_block, 1.0, 0.0)
+    for at in range(count):
+        blend = blend + jnp.where(numbers == chosen_ref[0, at], 1.0, 0.0)
+    bundle[cycles, :, 0:lane_count] = blend
     spread_rows = jnp.where(
         iota((rows, levels), 0) // block == iota((rows, levels), 1), 1.0, 0.0
     ).astype(jnp.bfloat16)
@@ -484,13 +511,29 @@
         tall = one(spread_rows, part).astype(jnp.bfloat16)
         kron[at] = jnp.where(same, one(tall, spread_rows, 1), 0.0).astype(jnp.bfloat16)
 
+    def meet():
+        pl.semaphore_wait(barrier, 2 * slab_count - 1 + 4)
+        copies = send_halo(0)
+
+        @pl.when(away == 1)
+        def _():
+            bundle_copy().start()
+
+        @pl.when(away == 0)
+        def _():
+            notes[...] = bundle[...]
+
+        return copies
+
     blend_copies = []
     for cycle in range(cycles):
         source = x_ref if cycle == 0 else returned
         if cycle:
             pack(source)
             copies = send_halo(cycle)
-        advance(source, cycle, copies)
+            advance(source, cycle, lambda: copies)
+        else:
+            advance(source, cycle, meet)
         heights_now = (h_ref, heights, send_h.at[cycle], recv_h.at[cycle])
         speeds_now = (u_ref, speeds, send_u.at[cycle], recv_u.at[cycle])
         drains = []
@@ -508,7 +551,7 @@
                 heights[slab] = h_ref[slab]
                 speeds[slab] = u_ref[slab]
 
-            blends[0] = notes[cycles, 0:8, 0 : blend_ref.shape[1]]
+            blends[0] = notes[cycles, 0:8, 0:lane_count]
             for step in range(1, grp_count):
                 copy = remote(
                     blends.at[0], blends.at[step], send_b.at[step], recv_b.at[step],
@@ -587,7 +630,10 @@
             inward_drain(0, *speeds_now)
     for field in (1, 0):
         outward_finish(field)
-    out_ref[...] = final[...]
+        for at in range(0, levels, 8):
+            part = final[field, at // slab_levels : (at + 8) // slab_levels]
+            part = part.reshape(8, block, width)
+            out_ref[:, field, at : at + 8] = jnp.swapaxes(part, 0, 1)
 
 
 def shards(ensemble, coupling, obs_column, obs_level, obs_value, obs_error, obs_live, partners):
@@ -595,36 +641,28 @@
     grp_count = lax.axis_size("grp")
     hor_count = lax.axis_size("hor")
     slab_count = mem_count * grp_count
-    own_slab = lax.axis_index("mem") * grp_count + lax.axis_index("grp")
-    lanes = max(128, -(-slab_count // 128) * 128)
-    slab_numbers = jnp.arange(lanes, dtype=jnp.int32)
-    chosen = partners[0, 0]
-    count = chosen.shape[0]
-    blend_weights = (slab_numbers == own_slab).astype(jnp.float32)
-    blend_weights = blend_weights + jnp.sum(
-        (slab_numbers[:, None] == chosen[None, :]).astype(jnp.float32), axis=1
-    )
-    blend = jnp.broadcast_to(blend_weights, (8, lanes))
+    lanes = max(LANES, -(-slab_count // LANES) * LANES)
+    count = partners.shape[-1]
     block, fields, levels, width = ensemble.shape
     cycles = obs_column.shape[0]
     members = block * slab_count
     slab_levels = levels // slab_count
-    x = ensemble.reshape(block, fields, slab_count, slab_levels, width).transpose(1, 2, 3, 0, 4)
     state = (slab_count, slab_levels, block, width)
     strip = (slab_count, slab_levels, block, LANES)
-    tall = (members + 8, members)
+    tall = (members // 2 + 8, members)
     rows = levels * block
     groups = 2 * levels * HALO // LANES
     slots = max(obs_column.shape[-1], lanes)
     vmem = pl.BlockSpec(memory_space=pltpu.VMEM)
     dma = pltpu.SemaphoreType.DMA
     f32 = jnp.float32
-    result = pl.pallas_call(
+    return pl.pallas_call(
         functools.partial(program, (mem_count, grp_count, hor_count), count, cycles),
-        out_shape=jax.ShapeDtypeStruct((2,) + state, f32),
-        in_specs=[vmem] * 8,
+        out_shape=jax.ShapeDtypeStruct(ensemble.shape, f32),
+        in_specs=[vmem] * 7 + [pl.BlockSpec(memory_space=pltpu.SMEM)],
         out_specs=vmem,
         scratch_shapes=[
+            pltpu.VMEM((2,) + state, f32),
             pltpu.VMEM((2, rows, rows), jnp.bfloat16),
             pltpu.VMEM(state, f32), pltpu.VMEM(state, f32), pltpu.VMEM(state, f32),
             pltpu.VMEM(strip, f32), pltpu.VMEM(strip, f32), pltpu.VMEM(strip, f32),
@@ -640,7 +678,7 @@
             pltpu.VMEM((mem_count - 1,) + tall, f32),
             pltpu.VMEM((grp_count - 1,) + tall, f32),
             pltpu.VMEM((grp_count - 1,) + tall, f32),
-            pltpu.VMEM((grp_count,) + blend.shape, f32),
+            pltpu.VMEM((grp_count, 8, lanes), f32),
             dma((cycles, 2)), dma((cycles, 2)),
             dma((1,)), dma((1,)),
             dma((cycles, mem_count - 1)), dma((cycles, mem_count - 1)),
@@ -654,10 +692,9 @@
         ],
         compiler_params=pltpu.CompilerParams(collective_id=0, has_side_effects=True),
     )(
-        x, coupling, obs_column[:, 0], obs_level[:, 0], obs_value[:, 0], obs_error[:, 0],
-        obs_live[:, 0], blend,
+        ensemble, coupling, obs_column[:, 0], obs_level[:, 0], obs_value[:, 0], obs_error[:, 0],
+        obs_live[:, 0], partners[0],
     )
-    return result.transpose(3, 0, 1, 2, 4).reshape(ensemble.shape)
 
 
 def solution(mesh):

time: 127 us -> 115 us (0.906)
  Pallas kernels: 119 us -> 112 us
  local copies, waits for them, and re-layouts: 6.86 us -> 2.29 us
    pallas_call x1, Pallas kernels: 119 us -> 112 us  [shards(): pl.pallas_call(functools.partial(program, (mem_count, grp_count, hor_coun...]
    reshape x1 -> x0, local copies, waits for them, and re-layouts: 2.81 us -> none  [shards(): return result.transpose(3, 0, 1, 2, 4).reshape(ensemble.shape)]
    unnamed x3 -> x1, local copies, waits for them, and re-layouts: 3.46 us -> 2.29 us
where the time goes in v3:
time: 115 us; the launch traced here: 114 us
  Pallas kernels  112 us (97%)
  local copies, waits for them, and re-layouts  2.29 us (2%)
    pallas_call x1, Pallas kernels, shards(): pl.pallas_call(functools.partial(program, (mem_count, grp_count, hor_coun...  112 us

profile of v3, /device:TPU:11, one launch (start us, length us, event | category | flops | bytes accessed | tf_op | source)
XLA Modules:
  0.0 114.4 jit_solution(7251693657514918343)
XLA Ops:
  0.0 112.1 %shard_map.82 = f32[8,2,32,512]{3,2,1,0:T(8,128)} custom-call(f32[8,2,32,512]{3,2,1,0:T(8,128)} %given_ref.1, f32[32,32]{1,0:T(8,128)} %coupling_ref.1, s32[2,1,512]{2,1,0:T(1,128)} %bitcast.6, s32[2,1,512]{2,1,0:T(1,128)} %bitcast.7, f32[2,1,512]{2,1,0:T(1,128)} %bitcast.8, f32[2,1,512]{2,1,0:T(1,128)} %bitcast.9, s32[2,1,512]{2,1,0:T(1,128)} %bitcast.10, ...), custom_call_target="tpu_custom_call" | custom-call | tf_op jit(solution)/shard_map/pallas_call | solution.py:659
  112.1 2.3 %copy.10 = f32[8,2,32,512]{3,2,1,0:T(8,128)} copy(f32[8,2,32,512]{3,2,1,0:T(8,128)} %shard_map.82) | data formatting | bytes 2097152

commit v4 on v3

--- a/solution.py
+++ b/solution.py
@@ -12,6 +12,7 @@
 MESH = pl.DeviceIdType.MESH
 LANES = 128
 HALO = 2 * SUBSTEPS
+EARLY = 1
 
 time_step = 0.2
 
@@ -48,8 +49,9 @@
 
 def program(
     sizes, count, cycles,
-    given_ref, coupling_ref, column_ref, level_ref, value_ref, error_ref, live_ref, chosen_ref,
+    given_hbm, coupling_hbm, column_hbm, level_hbm, value_hbm, error_hbm, live_hbm, chosen_ref,
     out_ref,
+    given_ref, coupling_ref, column_ref, level_ref, value_ref, error_ref, live_ref, fetch_sem,
     x_ref, kron, u_ref, h_ref, p_ref, edge_u, edge_h, edge_p, packed, halo,
     heights, speeds, updated, returned, final, relayed, cells, bundle, notes,
     own, column, partial, arrived, blends,
@@ -57,6 +59,15 @@
     send_h, recv_h, send_u, recv_u, send_e, recv_e, send_f, recv_f,
     send_r, recv_r, send_g,
 ):
+    fetches = []
+    for at, (source, target) in enumerate((
+        (given_hbm, given_ref), (coupling_hbm, coupling_ref), (column_hbm, column_ref),
+        (level_hbm, level_ref), (value_hbm, value_ref), (error_hbm, error_ref),
+        (live_hbm, live_ref),
+    )):
+        copy = pltpu.make_async_copy(source, target, fetch_sem.at[at])
+        copy.start()
+        fetches.append(copy)
     mem_count, grp_count, hor_count = sizes
     mem = lax.axis_index("mem")
     grp = lax.axis_index("grp")
@@ -94,6 +105,8 @@
         for one_side in range(2) for one_deep in range(depth) for one_grp in range(grp_count)
     ]
     cube = [spot(half, *step) for step in steps[:0:-1]]
+    level_first = [spot(half, *step) for step in steps[1:] if step[1] == 0]
+    level_later = [spot(half, *step) for step in steps[1:] if step[1]]
     across = [(at, spot(1 - half, 0, *step[1:])) for at, step in enumerate(steps[: len(steps) // 2])]
 
     right = ({"hor": turned(hor, 1, hor_count)},
@@ -173,8 +186,8 @@
                 mixed = jnp.where(lane < HALO, before, mixed)
                 target[place] = jnp.where(lane >= LANES - HALO, after, mixed)
 
-    def centred(field):
-        return (pltpu.roll(field, field.shape[-1] - 1, 1) - pltpu.roll(field, 1, 1)) * 0.5
+    def rise(field):
+        return pltpu.roll(field, field.shape[-1] - 1, 1) - pltpu.roll(field, 1, 1)
 
     def substep(read_u, read_h, write_u, write_h, press):
         span = press.shape[-1]
@@ -191,8 +204,8 @@
             velocity = read_u(part, everything).reshape(size)
             height = read_h(part, everything).reshape(size)
             pressure = press[part].reshape(size)
-            moved = velocity - time_step * (velocity * centred(velocity) + centred(pressure))
-            risen = height - time_step * centred(moved * height)
+            moved = velocity - 0.5 * time_step * (velocity * rise(velocity) + rise(pressure))
+            risen = height - 0.5 * time_step * rise(moved * height)
             write_u[part] = moved.reshape(1, slab_levels, block, span)
             write_h[part] = risen.reshape(1, slab_levels, block, span)
 
@@ -208,6 +221,13 @@
         def again(step, carry):
             substep(reader(u_ref), reader(h_ref), u_ref, h_ref, p_ref)
             return carry
+
+        def edge(step, carry):
+            substep(reader(edge_u), reader(edge_h), edge_u, edge_h, edge_p)
+            return carry
+
+        def both(step, carry):
+            return edge(step, again(step, carry))
 
         ahead = SUBSTEPS // 2 if cycle == 0 else 1
         if ahead > 1:
@@ -217,11 +237,6 @@
         for copy in copies:
             copy.wait()
         unpack(source, cycle)
-
-        def edge(step, carry):
-            substep(reader(edge_u), reader(edge_h), edge_u, edge_h, edge_p)
-            return carry
-
         lax.fori_loop(0, SUBSTEPS, edge, 0)
         lane = iota((block, LANES), 1)
         for strip, whole in ((edge_h, h_ref), (edge_u, u_ref)):
@@ -242,9 +257,9 @@
             target.at[other], target.at[other], recv_sem.at[other], recv_sem.at[other], {"hor": hor}
         ).wait_recv()
 
-    def cube_send(source, target, send_sem, recv_sem):
+    def cube_send(source, target, send_sem, recv_sem, some=slice(None)):
         copies = []
-        for device, other in cube:
+        for device, other in cube[some]:
             copy = remote(
                 source.at[other], target.at[slab], send_sem.at[other], recv_sem.at[slab], device
             )
@@ -285,17 +300,22 @@
             send_g.at[field, at], recv_sem.at[first_block], device,
         )
 
-    def inward_send(field, source, target, send_sem, recv_sem):
+    def inward_send(field, source, target, send_sem, recv_sem, early=True, late=True):
+        some = slice(0 if early else EARLY, None if late else EARLY)
+
         @pl.when(away == 1)
         def _():
-            for copy in inward_copies(straight, source, target, send_sem, recv_sem):
+            for copy in inward_copies(straight[some], source, target, send_sem, recv_sem):
                 copy.start()
 
         @pl.when(away == 0)
         def _():
-            for copy in inward_copies(cube, source, target, send_sem, recv_sem):
+            if early:
+                for copy in inward_copies(level_first, source, target, send_sem, recv_sem):
+                    copy.start()
+            own_copies = inward_copies(level_later[some], source, target, send_sem, recv_sem)
+            for copy, (at, (device, other)) in zip(own_copies, across[some]):
                 copy.start()
-            for at, (device, other) in across:
                 relay_copy(field, source, at, other).wait_recv()
                 forward_copy(field, target, recv_sem, at, device).start()
 
@@ -484,6 +504,8 @@
             )
             updated[field, :, level] = result.reshape(slab_count, block, width)
 
+    for copy in fetches:
+        copy.wait()
     for field in range(2):
         for at in range(0, levels, 8):
             part = given_ref[:, field, at : at + 8]
@@ -541,6 +563,7 @@
             inward_relay(1, h_ref)
             inward_send(1, *heights_now)
             inward_relay(0, u_ref)
+            inward_send(0, *speeds_now, late=False)
 
             @pl.when(away == 1)
             def _():
@@ -560,7 +583,7 @@
                 copy.start()
                 blend_copies.append(copy)
         else:
-            drains = cube_send(*heights_now)
+            drains = cube_send(*heights_now) + cube_send(*speeds_now, slice(0, 2 * EARLY))
             heights[slab] = h_ref[slab]
             speeds[slab] = u_ref[slab]
         sum_cells(cycle)
@@ -580,9 +603,9 @@
             copy.start()
             gathers.append(copy)
         if cycle == 0:
-            inward_send(0, *speeds_now)
+            inward_send(0, *speeds_now, early=False)
         else:
-            drains = drains + cube_send(*speeds_now)
+            drains = drains + cube_send(*speeds_now, slice(2 * EARLY, None))
         for copy in blend_copies:
             copy.wait()
         blend_copies = []
@@ -652,6 +675,7 @@
     tall = (members // 2 + 8, members)
     rows = levels * block
     groups = 2 * levels * HALO // LANES
+    noted = (cycles, 1, obs_column.shape[-1])
     slots = max(obs_column.shape[-1], lanes)
     vmem = pl.BlockSpec(memory_space=pltpu.VMEM)
     dma = pltpu.SemaphoreType.DMA
@@ -659,9 +683,13 @@
     return pl.pallas_call(
         functools.partial(program, (mem_count, grp_count, hor_count), count, cycles),
         out_shape=jax.ShapeDtypeStruct(ensemble.shape, f32),
-        in_specs=[vmem] * 7 + [pl.BlockSpec(memory_space=pltpu.SMEM)],
+        in_specs=[pl.BlockSpec(memory_space=pltpu.HBM)] * 7 + [pl.BlockSpec(memory_space=pltpu.SMEM)],
         out_specs=vmem,
         scratch_shapes=[
+            pltpu.VMEM(ensemble.shape, f32), pltpu.VMEM(coupling.shape, f32),
+            pltpu.VMEM(noted, jnp.int32), pltpu.VMEM(noted, jnp.int32),
+            pltpu.VMEM(noted, f32), pltpu.VMEM(noted, f32), pltpu.VMEM(noted, jnp.int32),
+            dma((7,)),
             pltpu.VMEM((2,) + state, f32),
             pltpu.VMEM((2, rows, rows), jnp.bfloat16),
             pltpu.VMEM(state, f32), pltpu.VMEM(state, f32), pltpu.VMEM(state, f32),

time: 115 us -> 114 us (level)
  no operation moved by 1% of the time
where the time goes in v4:
time: 114 us
  Pallas kernels  111 us (97%)
  local copies, waits for them, and re-layouts  2.29 us (2%)
    pallas_call x1, Pallas kernels, shards(): pl.pallas_call(functools.partial(program, (mem_count, grp_count, hor_coun...  111 us
    unnamed x1, local copies, waits for them, and re-layouts  2.29 us

profile of v4, /device:TPU:11, one launch (start us, length us, event | category | flops | bytes accessed | tf_op | source)
XLA Modules:
  0.0 113.7 jit_solution(11885089490644903766)
XLA Ops:
  0.0 111.4 %shard_map.82 = f32[8,2,32,512]{3,2,1,0:T(8,128)} custom-call(f32[8,2,32,512]{3,2,1,0:T(8,128)} %given_hbm.1, f32[32,32]{1,0:T(8,128)} %coupling_hbm.1, s32[2,1,512]{2,1,0:T(1,128)} %bitcast.6, s32[2,1,512]{2,1,0:T(1,128)} %bitcast.7, f32[2,1,512]{2,1,0:T(1,128)} %bitcast.8, f32[2,1,512]{2,1,0:T(1,128)} %bitcast.9, s32[2,1,512]{2,1,0:T(1,128)} %bitcast.10, ...), custom_call_target="tpu_custom_call" | custom-call | tf_op jit(solution)/shard_map/pallas_call | solution.py:683
  111.4 2.3 %copy.10 = f32[8,2,32,512]{3,2,1,0:T(8,128)} copy(f32[8,2,32,512]{3,2,1,0:T(8,128)} %shard_map.82) | data formatting | bytes 2097152

commit v5 on v4

--- a/solution.py
+++ b/solution.py
@@ -50,10 +50,10 @@
 def program(
     sizes, count, cycles,
     given_hbm, coupling_hbm, column_hbm, level_hbm, value_hbm, error_hbm, live_hbm, chosen_ref,
-    out_ref,
+    final_hbm,
     given_ref, coupling_ref, column_ref, level_ref, value_ref, error_ref, live_ref, fetch_sem,
     x_ref, kron, u_ref, h_ref, p_ref, edge_u, edge_h, edge_p, packed, halo,
-    heights, speeds, updated, returned, final, relayed, cells, bundle, notes,
+    heights, speeds, updated, returned, relayed, cells, bundle, notes,
     own, column, partial, arrived, blends,
     send_n, recv_n, send_o, recv_o, send_a, recv_a, send_b, recv_b, send_c, recv_c,
     send_h, recv_h, send_u, recv_u, send_e, recv_e, send_f, recv_f,
@@ -353,12 +353,17 @@
                 to_grp = turned(grp, step_grp, grp_count)
                 other = to_mem * grp_count + to_grp
                 copies.append(remote(
-                    updated.at[field, other], final.at[field, slab],
+                    updated.at[field, other], final_hbm.at[field, slab],
                     send_f.at[field, other], recv_f.at[field, slab],
                     {"mem": to_mem, "hor": 2 * pair + half, "grp": to_grp},
                 ))
         return copies
 
+    def keep_copy(field):
+        return pltpu.make_async_copy(
+            updated.at[field, slab], final_hbm.at[field, slab], send_f.at[field, slab]
+        )
+
     def outward_send(field):
         copies = outward_copies(field)
 
@@ -371,22 +376,26 @@
 
         @pl.when(away == 0)
         def _():
-            final[field, slab] = updated[field, slab]
+            keep_copy(field).start()
 
     def outward_finish(field):
         for at in range(slab_count):
             other = turned(slab, at, slab_count)
             if at:
-                arrive(final.at[field], recv_f.at[field], other)
+                arrive(final_hbm.at[field], recv_f.at[field], other)
             else:
                 @pl.when(away == 1)
                 def _():
-                    arrive(final.at[field], recv_f.at[field], other)
+                    arrive(final_hbm.at[field], recv_f.at[field], other)
         copies = outward_copies(field)
 
         @pl.when(away == 1)
         def _():
             copies[0].wait_send()
+
+        @pl.when(away == 0)
+        def _():
+            keep_copy(field).wait()
 
         for copy in copies[1:]:
             copy.wait_send()
@@ -487,9 +496,10 @@
         for step in range(1, ROOT_STEPS):
             iterate = product(newton, iterate)
             newton = 1.5 * identity - 0.5 * product(inverse_root, iterate)
+            if step == ROOT_STEPS - 1:
+                inner = product(product(bvector, newton), inverse_root)
             inverse_root = product(newton, inverse_root)
         spread = inverse_root * (jnp.sqrt(members - 1.0) / jnp.sqrt(frobenius))
-        inner = product(bvector, inverse_root)
         mean_weight = product(inner, inverse_root) / frobenius
         return spread + mean_weight[0:1]
 
@@ -504,16 +514,8 @@
             )
             updated[field, :, level] = result.reshape(slab_count, block, width)
 
-    for copy in fetches:
+    for copy in fetches[1:]:
         copy.wait()
-    for field in range(2):
-        for at in range(0, levels, 8):
-            part = given_ref[:, field, at : at + 8]
-            part = jnp.swapaxes(part, 0, 1)
-            x_ref[field, at // slab_levels : (at + 8) // slab_levels] = part.reshape(
-                8 // slab_levels, slab_levels, block, width
-            )
-    pack(x_ref)
     for cycle in range(cycles):
         weight = live_ref[cycle].astype(jnp.float32) / error_ref[cycle]
         place = level_ref[cycle] * width + column_ref[cycle]
@@ -532,6 +534,15 @@
     for at, part in enumerate(split(coupling_ref[...])):
         tall = one(spread_rows, part).astype(jnp.bfloat16)
         kron[at] = jnp.where(same, one(tall, spread_rows, 1), 0.0).astype(jnp.bfloat16)
+    fetches[0].wait()
+    for field in range(2):
+        for at in range(0, levels, 8):
+            part = given_ref[:, field, at : at + 8]
+            part = jnp.swapaxes(part, 0, 1)
+            x_ref[field, at // slab_levels : (at + 8) // slab_levels] = part.reshape(
+                8 // slab_levels, slab_levels, block, width
+            )
+    pack(x_ref)
 
     def meet():
         pl.semaphore_wait(barrier, 2 * slab_count - 1 + 4)
@@ -653,10 +664,32 @@
             inward_drain(0, *speeds_now)
     for field in (1, 0):
         outward_finish(field)
-        for at in range(0, levels, 8):
-            part = final[field, at // slab_levels : (at + 8) // slab_levels]
-            part = part.reshape(8, block, width)
-            out_ref[:, field, at : at + 8] = jnp.swapaxes(part, 0, 1)
+
+
+def turn(state_hbm, out_hbm, given, turned, read_sem, write_sem):
+    fields, slab_count, slab_levels, block, width = given.shape
+    per = 8 // slab_levels
+    parts = [(field, at) for field in (1, 0) for at in range(0, slab_count, per)]
+    reads, writes = [], []
+    for number, (field, at) in enumerate(parts):
+        copy = pltpu.make_async_copy(
+            state_hbm.at[field, at : at + per], given.at[field, at : at + per],
+            read_sem.at[number],
+        )
+        copy.start()
+        reads.append(copy)
+    for number, (field, at) in enumerate(parts):
+        reads[number].wait()
+        levels = slice(at * slab_levels, (at + per) * slab_levels)
+        part = given[field, at : at + per].reshape(8, block, width)
+        turned[:, field, levels] = jnp.swapaxes(part, 0, 1)
+        copy = pltpu.make_async_copy(
+            turned.at[:, field, levels], out_hbm.at[:, field, levels], write_sem.at[number]
+        )
+        copy.start()
+        writes.append(copy)
+    for copy in writes:
+        copy.wait()
 
 
 def shards(ensemble, coupling, obs_column, obs_level, obs_value, obs_error, obs_live, partners):
@@ -680,11 +713,11 @@
     vmem = pl.BlockSpec(memory_space=pltpu.VMEM)
     dma = pltpu.SemaphoreType.DMA
     f32 = jnp.float32
-    return pl.pallas_call(
+    result = pl.pallas_call(
         functools.partial(program, (mem_count, grp_count, hor_count), count, cycles),
-        out_shape=jax.ShapeDtypeStruct(ensemble.shape, f32),
+        out_shape=jax.ShapeDtypeStruct((2,) + state, f32),
         in_specs=[pl.BlockSpec(memory_space=pltpu.HBM)] * 7 + [pl.BlockSpec(memory_space=pltpu.SMEM)],
-        out_specs=vmem,
+        out_specs=pl.BlockSpec(memory_space=pl.ANY),
         scratch_shapes=[
             pltpu.VMEM(ensemble.shape, f32), pltpu.VMEM(coupling.shape, f32),
             pltpu.VMEM(noted, jnp.int32), pltpu.VMEM(noted, jnp.int32),
@@ -698,7 +731,6 @@
             pltpu.VMEM((cycles, 2, groups, block, LANES), f32),
             pltpu.VMEM(state, f32), pltpu.VMEM(state, f32),
             pltpu.VMEM((2,) + state, f32), pltpu.VMEM((2,) + state, f32),
-            pltpu.VMEM((2,) + state, f32),
             pltpu.VMEM((2, slab_count // 2) + state[1:], f32),
             pltpu.VMEM((2, slab_levels * width // LANES, 1, LANES), f32),
             pltpu.VMEM((cycles + 1, 8, slots), f32), pltpu.VMEM((cycles + 1, 8, slots), f32),
@@ -723,6 +755,17 @@
         ensemble, coupling, obs_column[:, 0], obs_level[:, 0], obs_value[:, 0], obs_error[:, 0],
         obs_live[:, 0], partners[0],
     )
+    anywhere = pl.BlockSpec(memory_space=pl.ANY)
+    parts = 2 * levels // 8
+    return pl.pallas_call(
+        turn,
+        out_shape=jax.ShapeDtypeStruct(ensemble.shape, f32),
+        in_specs=[anywhere], out_specs=anywhere,
+        scratch_shapes=[
+            pltpu.VMEM((2,) + state, f32), pltpu.VMEM(ensemble.shape, f32),
+            dma((parts,)), dma((parts,)),
+        ],
+    )(result)
 
 
 def solution(mesh):

time: 114 us -> 113 us (level)
  local copies, waits for them, and re-layouts: 2.29 us -> 0 us
  Pallas kernels: 111 us -> 113 us
    unnamed x1 -> x0, local copies, waits for them, and re-layouts: 2.29 us -> none
    pallas_call x0 -> x1, Pallas kernels: none -> 2.11 us  [shards(): pl.pallas_call(turn, out_shape=jax.ShapeDtypeStruct(ensemble.shape, f32),...]
where the time goes in v5:
time: 113 us
  Pallas kernels  113 us (100%)
    pallas_call x1, Pallas kernels, shards(): pl.pallas_call(functools.partial(program, (mem_count, grp_count, hor_coun...  111 us

profile of v5, /device:TPU:11, one launch (start us, length us, event | category | flops | bytes accessed | tf_op | source)
XLA Modules:
  0.0 113.0 jit_solution(9372924268878313513)
XLA Ops:
  0.0 110.7 %shard_map.82.state_hbm = f32[2,16,2,8,512]{4,3,2,1,0:T(8,128)} custom-call(f32[8,2,32,512]{3,2,1,0:T(8,128)} %given_hbm.1, f32[32,32]{1,0:T(8,128)} %coupling_hbm.1, s32[2,1,512]{2,1,0:T(1,128)} %bitcast.6, s32[2,1,512]{2,1,0:T(1,128)} %bitcast.7, f32[2,1,512]{2,1,0:T(1,128)} %bitcast.8, f32[2,1,512]{2,1,0:T(1,128)} %bitcast.9, s32[2,1,512]{2,1,0:T(1,128)} %bitcast.10, ...), custom_call_target="tpu_custom_call" | custom-call | tf_op jit(solution)/shard_map/pallas_call | solution.py:716
  110.7 2.1 %shard_map.83 = f32[8,2,32,512]{3,2,1,0:T(8,128)} custom-call(f32[2,16,2,8,512]{4,3,2,1,0:T(8,128)} %shard_map.82.state_hbm), custom_call_target="tpu_custom_call" | custom-call | tf_op jit(solution)/shard_map/pallas_call | solution.py:760

commit v6 on v5

--- a/solution.py
+++ b/solution.py
@@ -229,7 +229,7 @@
         def both(step, carry):
             return edge(step, again(step, carry))
 
-        ahead = SUBSTEPS // 2 if cycle == 0 else 1
+        ahead = 1
         if ahead > 1:
             lax.fori_loop(1, ahead, again, 0)
         copies = greet()
@@ -345,9 +345,11 @@
                     def _():
                         arrive(target, recv_sem, other)
 
+    crossing = [(at + depth) % mem_count for at in range(mem_count) if at != depth]
+
     def outward_copies(field):
         copies = []
-        for step_mem in range(mem_count):
+        for step_mem in [0] + crossing:
             for step_grp in range(grp_count):
                 to_mem = turned(mem, step_mem, mem_count)
                 to_grp = turned(grp, step_grp, grp_count)

time: 113 us -> 113 us (level)
  no operation moved by 1% of the time
where the time goes in v6:
time: 113 us; the launch traced here: 112 us
  Pallas kernels  112 us (99%)
    pallas_call x1, Pallas kernels, shards(): pl.pallas_call(functools.partial(program, (mem_count, grp_count, hor_coun...  110 us

profile of v6, /device:TPU:11, one launch (start us, length us, event | category | flops | bytes accessed | tf_op | source)
XLA Modules:
  0.0 112.5 jit_solution(2749611158180773221)
XLA Ops:
  0.0 110.2 %shard_map.82.state_hbm = f32[2,16,2,8,512]{4,3,2,1,0:T(8,128)} custom-call(f32[8,2,32,512]{3,2,1,0:T(8,128)} %given_hbm.1, f32[32,32]{1,0:T(8,128)} %coupling_hbm.1, s32[2,1,512]{2,1,0:T(1,128)} %bitcast.6, s32[2,1,512]{2,1,0:T(1,128)} %bitcast.7, f32[2,1,512]{2,1,0:T(1,128)} %bitcast.8, f32[2,1,512]{2,1,0:T(1,128)} %bitcast.9, s32[2,1,512]{2,1,0:T(1,128)} %bitcast.10, ...), custom_call_target="tpu_custom_call" | custom-call | tf_op jit(solution)/shard_map/pallas_call | solution.py:718
  110.2 2.1 %shard_map.83 = f32[8,2,32,512]{3,2,1,0:T(8,128)} custom-call(f32[2,16,2,8,512]{4,3,2,1,0:T(8,128)} %shard_map.82.state_hbm), custom_call_target="tpu_custom_call" | custom-call | tf_op jit(solution)/shard_map/pallas_call | solution.py:762

commit v7 on v6

--- a/solution.py
+++ b/solution.py
@@ -238,19 +238,21 @@
             copy.wait()
         unpack(source, cycle)
         lax.fori_loop(0, SUBSTEPS, edge, 0)
+        mend(edge_h, h_ref)
+
+    def mend(strip, whole):
         lane = iota((block, LANES), 1)
-        for strip, whole in ((edge_h, h_ref), (edge_u, u_ref)):
-            for at in range(slab_count):
-                for level in range(slab_levels):
-                    fresh = strip[at, level]
-                    first = whole[at, level, :, 0:LANES]
-                    last = whole[at, level, :, width - LANES : width]
-                    whole[at, level, :, 0:LANES] = jnp.where(
-                        lane < HALO, pltpu.roll(fresh, LANES - HALO, 1), first
-                    )
-                    whole[at, level, :, width - LANES : width] = jnp.where(
-                        lane >= LANES - HALO, pltpu.roll(fresh, HALO, 1), last
-                    )
+        for at in range(slab_count):
+            for level in range(slab_levels):
+                fresh = strip[at, level]
+                first = whole[at, level, :, 0:LANES]
+                last = whole[at, level, :, width - LANES : width]
+                whole[at, level, :, 0:LANES] = jnp.where(
+                    lane < HALO, pltpu.roll(fresh, LANES - HALO, 1), first
+                )
+                whole[at, level, :, width - LANES : width] = jnp.where(
+                    lane >= LANES - HALO, pltpu.roll(fresh, HALO, 1), last
+                )
 
     def arrive(target, recv_sem, other):
         remote(
@@ -575,6 +577,7 @@
         if cycle == 0:
             inward_relay(1, h_ref)
             inward_send(1, *heights_now)
+            mend(edge_u, u_ref)
             inward_relay(0, u_ref)
             inward_send(0, *speeds_now, late=False)
 
@@ -596,7 +599,9 @@
                 copy.start()
                 blend_copies.append(copy)
         else:
-            drains = cube_send(*heights_now) + cube_send(*speeds_now, slice(0, 2 * EARLY))
+            drains = cube_send(*heights_now)
+            mend(edge_u, u_ref)
+            drains = drains + cube_send(*speeds_now, slice(0, 2 * EARLY))
             heights[slab] = h_ref[slab]
             speeds[slab] = u_ref[slab]
         sum_cells(cycle)

time: 113 us -> 113 us (level)
  no operation moved by 1% of the time
where the time goes in v7:
time: 113 us; the launch traced here: 112 us
  Pallas kernels  112 us (99%)
    pallas_call x1, Pallas kernels, shards(): pl.pallas_call(functools.partial(program, (mem_count, grp_count, hor_coun...  110 us

profile of v7, /device:TPU:11, one launch (start us, length us, event | category | flops | bytes accessed | tf_op | source)
XLA Modules:
  0.0 112.3 jit_solution(10914280233465732753)
XLA Ops:
  0.0 110.0 %shard_map.82.state_hbm = f32[2,16,2,8,512]{4,3,2,1,0:T(8,128)} custom-call(f32[8,2,32,512]{3,2,1,0:T(8,128)} %given_hbm.1, f32[32,32]{1,0:T(8,128)} %coupling_hbm.1, s32[2,1,512]{2,1,0:T(1,128)} %bitcast.6, s32[2,1,512]{2,1,0:T(1,128)} %bitcast.7, f32[2,1,512]{2,1,0:T(1,128)} %bitcast.8, f32[2,1,512]{2,1,0:T(1,128)} %bitcast.9, s32[2,1,512]{2,1,0:T(1,128)} %bitcast.10, ...), custom_call_target="tpu_custom_call" | custom-call | tf_op jit(solution)/shard_map/pallas_call | solution.py:723
  110.0 2.1 %shard_map.83 = f32[8,2,32,512]{3,2,1,0:T(8,128)} custom-call(f32[2,16,2,8,512]{4,3,2,1,0:T(8,128)} %shard_map.82.state_hbm), custom_call_target="tpu_custom_call" | custom-call | tf_op jit(solution)/shard_map/pallas_call | solution.py:767
